TPU v7x, 16 devices: a 4x2x1 block of a 4x4x8 slice. The times are simulated.
16 devices in a mesh: dp: 2 (over y, z), ep: 8 (over x, core).
Axes of the slice: x: 4, y: 2, z: 1, core: 2. Of those that a mesh axis runs over, the one named last changes fastest.
The devices are a block of a 4x4x8 slice.
Arguments:
- tokens: bfloat16 [131072, 768], P(('dp', 'ep')), parts along dimension 0
- choice_idx: int32 [64, 2048], P(('dp', 'ep')), parts along dimension 0
- gate_weight: float32 [64, 2048], P(('dp', 'ep')), parts along dimension 0
- w_in: bfloat16 [32, 768, 3072], P('ep')
- w_out: bfloat16 [32, 3072, 768], P('ep')
Outputs:
- output: bfloat16 [131072, 768], P(('dp', 'ep')), parts along dimension 0
There are 2 independent parts. A program takes and returns all parts, laid end to end along the dimension named above; an argument that names none is the same for every part.
All inputs are finite; a program needn't handle non-finite values.
Results may differ from a plain program's by a relative error of at most 0.001.
Values are sent between devices in bfloat16 or wider.
A program may use at most 768 MiB of HBM per device.

v0:
```python
import jax
import jax.numpy as jnp
from jax import lax
from jax.sharding import PartitionSpec as P


def solution(mesh):
    group_n = mesh.shape["ep"]
    row_spec = P(("dp", "ep"), None)
    expert_spec = P("ep", None, None)

    def local_layer(tok_loc, sel_loc, gate_loc, win_loc, wout_loc):
        tok_count, model_dim = tok_loc.shape
        exp_count, cap_slots = sel_loc.shape
        slot_total = exp_count * cap_slots
        pair_cap = 2 * slot_total // group_n
        flat_sel = sel_loc.reshape(slot_total)
        src_dev = flat_sel // tok_count
        src_row = flat_sel % tok_count
        slot_order = jnp.argsort(src_dev, stable=True)
        counts = jax.ops.segment_sum(jnp.ones_like(src_dev), src_dev, num_segments=group_n)
        starts = jnp.cumsum(counts) - counts
        lane_idx = jnp.arange(pair_cap, dtype=jnp.int32)
        is_valid = lane_idx[None, :] < counts[:, None]
        slot_of = slot_order[jnp.minimum(starts[:, None] + lane_idx[None, :], slot_total - 1)]
        request = jnp.where(is_valid, src_row[slot_of], 0)
        sorted_rank = jnp.zeros(slot_total, jnp.int32).at[slot_order].set(jnp.arange(slot_total, dtype=jnp.int32))
        recv_place = src_dev * pair_cap + sorted_rank - starts[src_dev]
        asked_rows = lax.all_to_all(request, "ep", 0, 0, tiled=True)
        send_rows = tok_loc[asked_rows]
        got_rows = lax.all_to_all(send_rows, "ep", 0, 0, tiled=True)
        expert_in = got_rows.reshape(group_n * pair_cap, model_dim)[recv_place].reshape(exp_count, cap_slots, model_dim)
        pre_act = jnp.einsum("ecd,edf->ecf", expert_in, win_loc, preferred_element_type=jnp.float32)
        hidden = jax.nn.gelu(pre_act, approximate=True).astype(jnp.bfloat16)
        expert_out = jnp.einsum("ecf,efd->ecd", hidden, wout_loc, preferred_element_type=jnp.float32)
        weighted = (gate_loc[:, :, None] * expert_out).astype(jnp.bfloat16).reshape(slot_total, model_dim)
        back_rows = jnp.where(is_valid[:, :, None], weighted[slot_of], jnp.zeros((), jnp.bfloat16))
        returned = lax.all_to_all(back_rows, "ep", 0, 0, tiled=True)
        added = jax.ops.segment_sum(returned.reshape(group_n * pair_cap, model_dim).astype(jnp.float32), asked_rows.reshape(group_n * pair_cap), num_segments=tok_count)
        return (tok_loc.astype(jnp.float32) + added).astype(jnp.bfloat16)

    return jax.shard_map(local_layer, mesh=mesh, in_specs=(row_spec, row_spec, row_spec, expert_spec, expert_spec), out_specs=row_spec, check_vma=False)
```

profile of v0, /device:TPU:112, one launch (start us, length us, event | category | flops | bytes accessed | tf_op | source)
XLA Modules:
  0.0 1343.7 jit_solution(4547879704410136286)
XLA Ops:
  0.0 0.8 copy.6
  0.8 0.3 compare_reduce_fusion
  1.1 57.0 %scatter_custom_fusion = s32[8]{0:T(128)S(1)} fusion(s32[8192]{0:T(1024)S(1)} %bitcast.71, s32[8192]{0:T(1024)S(1)} %broadcast.249, s32[]{:T(128)} %constant.18.clone.1), kind=kCustom, calls=%fused_computation.56 | custom fusion | flops 8192 | bytes 36 | tf_op jit(solution)/shard_map/scatter-add | solution.py:21
  58.1 0.2 reduce-window.9
  58.3 0.7 fusion.17
  59.0 0.2 compare_select_fusion.2
  59.1 0.8 copy.7
  59.9 6.8 sort.17
  66.7 90.5 %gather_fusion = s32[16384]{0:T(1024)S(1)} fusion(s32[8192]{0:T(1024)S(1)} %get-tuple-element.6, s32[16384]{0:T(1024)S(1)} %broadcast_clamp_fusion.1), kind=kCustom, calls=%fused_computation | custom fusion | bytes 196608 | tf_op jit(solution)/shard_map/gather | solution.py:25
  157.3 0.1 compare_select_fusion.1
  157.4 0.0 copy-start
  157.4 30.5 %scatter_custom_fusion.1 = s32[8192]{0:T(1024)S(1)} fusion(s32[8192]{0:T(1024)S(1)} %compare_select_fusion.12, s32[8192]{0:T(1024)S(1)} %iota.21, s32[]{:T(128)} %constant.18.clone.1), kind=kCustom, calls=%fused_computation.53 | custom fusion | bytes 32772 | tf_op jit(solution)/shard_map/scatter | solution.py:27
  187.9 4.4 compare_select_fusion.5
  192.3 0.7 fusion.10
  193.1 90.5 %gather_fusion.1 = s32[16384]{0:T(1024)S(1)} fusion(s32[8192]{0:T(1024)S(1)} %get-tuple-element.10, s32[16384]{0:T(1024)S(1)} %broadcast_clamp_fusion.2), kind=kCustom, calls=%fused_computation.1 | custom fusion | bytes 196608 | tf_op jit(solution)/shard_map/gather | solution.py:26
  283.6 0.0 copy-done
  283.6 0.1 compare_select_fusion.3
  283.7 10.7 all_to_all.19
  294.5 0.0 copy-start.2
  294.5 0.6 copy-done.2
  295.1 0.1 compare_select_fusion
  295.2 79.2 %gather_fusion.2 = bf16[16384,768]{1,0:T(8,128)(2,1)} fusion(bf16[8192,768]{1,0:T(8,128)(2,1)} %param.5, s32[16384]{0:T(1024)S(1)} %broadcast_clamp_fusion), kind=kCustom, calls=%fused_computation.2 | custom fusion | bytes 50397184 | tf_op jit(solution)/shard_map/gather | solution.py:30
  374.4 6.8 all-to-all-start.1
  381.2 0.7 iota_compare_fusion
  381.9 273.5 %all-to-all-done.1 = bf16[8,2048,768]{2,1,0:T(8,128)(2,1)} async-done(((bf16[8,2048,768]{2,1,0:T(8,128)(2,1)}), bf16[8,2048,768]{2,1,0:T(8,128)(2,1)}, u32[]{:S(2)}, u32[]{:S(2)}) %all-to-all-start.1) | async-done | bytes 25165856 | tf_op jit(solution)/shard_map/all_to_all | solution.py:31
  655.4 48.4 %gather_fusion.3 = bf16[8192,768]{1,0:T(8,128)(2,1)} fusion(bf16[16384,768]{1,0:T(8,128)(2,1)} %bitcast.11, s32[8192]{0:T(1024)S(1)} %get-tuple-element.9), kind=kCustom, calls=%fused_computation.3 | custom fusion | bytes 25198592 | tf_op jit(solution)/shard_map/gather | solution.py:32
  703.8 0.0 copy-start.4
  703.8 66.4 %fusion.39 = bf16[4,2048,3072]{2,1,0:T(8,128)(2,1)} fusion(bf16[4,768,3072]{2,1,0:T(8,128)(2,1)} %param.8, bf16[4,2048,768]{2,1,0:T(8,128)(2,1)} %bitcast.60), kind=kOutput, calls=%bitcast_fusion.1.clone.1 | convolution fusion | flops 38881198080 | bytes 81788928 | tf_op jit(solution)/shard_map/ecd,edf->ecf/dot_general | solution.py:33
  770.2 0.0 copy-done.4
  770.2 0.0 copy-start.1
  770.2 48.2 %multiply_convert_fusion = bf16[4,2048,768]{2,1,0:T(8,128)(2,1)} fusion(f32[4,2048]{1,0:T(4,128)S(1)} %copy-done.4, bf16[4,3072,768]{2,1,0:T(8,128)(2,1)} %param.9, bf16[4,2048,3072]{2,1,0:T(8,128)(2,1)} %fusion.39), kind=kOutput, calls=%fused_computation.19 | convolution fusion | flops 38667288576 | bytes 81821696 | tf_op jit(solution)/shard_map/ecf,efd->ecd/dot_general | solution.py:35
  818.3 0.0 copy-done.1
  818.3 0.0 copy-start.3
  818.3 79.3 %gather_fusion.4 = bf16[16384,768]{1,0:T(8,128)(2,1)} fusion(bf16[8192,768]{1,0:T(8,128)(2,1)} %bitcast.57, s32[16384]{0:T(1024)S(1)} %copy-done.1), kind=kCustom, calls=%fused_computation.4 | custom fusion | bytes 50397184 | tf_op jit(solution)/shard_map/gather | solution.py:37
  897.6 0.0 copy-done.3
  897.7 22.2 %broadcast_select_fusion = bf16[8,2048,768]{2,1,0:T(8,128)(2,1)} fusion(bf16[8,2048,768]{2,1,0:T(8,128)(2,1)} %bitcast.59, pred[8,2048]{1,0:T(8,128)(4,1)S(1)} %copy-done.3), kind=kLoop, calls=%fused_computation.20 | loop fusion | flops 12582912 | bytes 50348032 | tf_op jit(solution)/shard_map/jit(_where)/select_n | solution.py:37
  919.8 6.9 all-to-all-start.2
  926.7 14.3 %convert_element_type.18 = f32[8192,768]{1,0:T(8,128)} convert(bf16[8192,768]{1,0:T(8,128)(2,1)} %param.5) | non-fusion elementwise | flops 6291456 | bytes 37748736 | tf_op jit(solution)/shard_map/convert_element_type | solution.py:40
  941.0 259.8 %all-to-all-done.2 = bf16[8,2048,768]{2,1,0:T(8,128)(2,1)} async-done(((bf16[8,2048,768]{2,1,0:T(8,128)(2,1)}), bf16[8,2048,768]{2,1,0:T(8,128)(2,1)}, u32[]{:S(2)}, u32[]{:S(2)}) %all-to-all-start.2) | async-done | bytes 25165856 | tf_op jit(solution)/shard_map/all_to_all | solution.py:38
  1200.8 129.4 %scatter_custom_fusion.2 = f32[8192,768]{1,0:T(8,128)} fusion(f32[8192,768]{1,0:T(8,128)} %convert_element_type.18, s32[16384]{0:T(1024)} %bitcast.63, bf16[16384,768]{1,0:T(8,128)(2,1)} %bitcast.25), kind=kCustom, calls=%fused_computation.17 | custom fusion | flops 25165824 | bytes 50331648 | tf_op jit(solution)/shard_map/scatter-add | solution.py:39
  1330.2 13.1 convert_element_type.23
  (9 shorter events, 0.1 us)
Async XLA Ops:
  157.4 126.2 %copy-start = (s32[16384]{0:T(1024)}, s32[16384]{0:T(1024)S(1)}, u32[]{:S(2)}) copy-start(s32[16384]{0:T(1024)S(1)} %broadcast_clamp_fusion.2) | copy-start | bytes 196612
  294.5 0.6 copy-start.2
  374.4 281.0 %all-to-all-start.1 = ((bf16[8,2048,768]{2,1,0:T(8,128)(2,1)}), bf16[8,2048,768]{2,1,0:T(8,128)(2,1)}, u32[]{:S(2)}, u32[]{:S(2)}) async-start(bf16[8,2048,768]{2,1,0:T(8,128)(2,1)} %bitcast.58), calls=%async_computation.1 | async-start | bytes 50331648 | tf_op jit(solution)/shard_map/all_to_all | solution.py:31
  703.8 66.4 %copy-start.4 = (f32[4,2048]{1,0:T(4,128)S(1)}, f32[4,2048]{1,0:T(4,128)}, u32[]{:S(2)}) copy-start(f32[4,2048]{1,0:T(4,128)} %param.7) | copy-start | bytes 98308
  770.2 48.2 %copy-start.1 = (s32[16384]{0:T(1024)S(1)}, s32[16384]{0:T(1024)}, u32[]{:S(2)}) copy-start(s32[16384]{0:T(1024)} %copy-done) | copy-start | bytes 196612
  818.3 79.3 %copy-start.3 = (pred[8,2048]{1,0:T(8,128)(4,1)S(1)}, pred[8,2048]{1,0:T(8,128)(4,1)}, u32[]{:S(2)}) copy-start(pred[8,2048]{1,0:T(8,128)(4,1)} %iota_compare_fusion) | copy-start | bytes 49156
  919.8 281.0 %all-to-all-start.2 = ((bf16[8,2048,768]{2,1,0:T(8,128)(2,1)}), bf16[8,2048,768]{2,1,0:T(8,128)(2,1)}, u32[]{:S(2)}, u32[]{:S(2)}) async-start(bf16[8,2048,768]{2,1,0:T(8,128)(2,1)} %broadcast_select_fusion), calls=%async_computation.2 | async-start | bytes 50331648 | tf_op jit(solution)/shard_map/all_to_all | solution.py:38
where the time goes:
time: 1350 us; the launch traced here: 1340 us
  waiting for transfers between devices  533 us (39%)
  local copies, waits for them, and re-layouts  421 us (31%)
  other arithmetic  249 us (18%)
  matrix products  115 us (9%)
  starting transfers between devices  13.7 us (1%)
    all_to_all x1, waiting for transfers between devices, local_layer(): got_rows = lax.all_to_all(send_rows, 'ep', 0, 0, tiled=True)  273 us
    all_to_all x1, waiting for transfers between devices, local_layer(): returned = lax.all_to_all(back_rows, 'ep', 0, 0, tiled=True)  260 us
    scatter-add x1, other arithmetic, local_layer(): jax.ops.segment_sum(returned.reshape(group_n * pair_cap, model_dim).astyp...  129 us
    gather x1, local copies, waits for them, and re-layouts, local_layer(): request = jnp.where(is_valid, src_row[slot_of], 0)  90.5 us
    gather x1, local copies, waits for them, and re-layouts, local_layer(): slot_order[jnp.minimum(starts[:, None] + lane_idx[None, :], slot_total - 1)]  90.5 us
    gather x1, local copies, waits for them, and re-layouts, local_layer(): weighted[slot_of]  79.3 us
    gather x1, local copies, waits for them, and re-layouts, local_layer(): send_rows = tok_loc[asked_rows]  79.2 us
    dot_general x1, matrix products, local_layer(): jnp.einsum('ecd,edf->ecf', expert_in, win_loc, preferred_element_type=jnp...  66.4 us
  transfers between devices with their start and end apart: 2, of which 2 were waited for; matrix products, arithmetic and copies ran while one was open for 1% of the time, Pallas kernels for 0%

commit v1 on v0

v1 whole, which is shorter than its diff:
```python
import functools

import jax
import jax.numpy as jnp
from jax import lax
from jax.experimental import pallas as pl
from jax.experimental.pallas import tpu as pltpu
from jax.sharding import PartitionSpec as P

LANES = 128
SUB = 8
GROUP = 16
VMEM_LIMIT = 62 * 1024 * 1024
CHUNKS = 4
ROW_TILE = 256


def load_table(tok_ref, raw, table, sems, rows):
    total, width = tok_ref.shape
    parts = total // rows
    copies = [
        pltpu.make_async_copy(tok_ref.at[pl.ds(p * rows, rows)], raw.at[pl.ds(p * rows, rows)], sems.at[p])
        for p in range(parts)
    ]
    for copy in copies:
        copy.start()
    for p in range(parts):
        copies[p].wait()

        def convert(g, carry):
            base = pl.multiple_of(p * rows + g * GROUP, GROUP)
            for k in range(width // LANES):
                x = raw[pl.ds(base, GROUP), k * LANES:(k + 1) * LANES].astype(jnp.float32)
                table[pl.ds(base * SUB + k, GROUP, stride=SUB), :] = x
            return carry

        lax.fori_loop(0, rows // GROUP, convert, 0, unroll=2)


def gather_kernel(chunk, ask_ref, live_ref, tok_ref, out_ref, raw, table, stage, sems):
    total, width = tok_ref.shape
    peers, block, _ = out_ref.shape
    load_table(tok_ref, raw, table, sems, total // sems.shape[0])
    mask = 2 * total - 1

    def per_peer(d, carry):
        live = jnp.clip(live_ref[d] - chunk * block, 0, block)

        def group(g, carry2):
            base = pl.multiple_of(g * GROUP, GROUP)
            slot = pl.multiple_of((g % 4) * GROUP * SUB, GROUP * SUB)
            for i in range(GROUP):
                row = ask_ref[d, chunk * block + base + i] & mask
                stage[pl.ds(slot + i * SUB, SUB), :] = table[pl.ds(pl.multiple_of(row * SUB, SUB), SUB), :]
            for k in range(width // LANES):
                y = stage[pl.ds(slot + k, GROUP, stride=SUB), :]
                out_ref[d, pl.ds(base, GROUP), k * LANES:(k + 1) * LANES] = y.astype(jnp.bfloat16)
            return carry2

        return lax.fori_loop(0, pl.cdiv(live, GROUP), group, carry)

    lax.fori_loop(0, peers, per_peer, 0)


def ffn_kernel(bound_ref, x_ref, gate_ref, win_ref, wout_ref, out_ref, w1, w2, hidden, sems):
    experts, width, inner = win_ref.shape
    peers, block, _ = x_ref.shape
    tile = hidden.shape[0]
    cut = 512

    def fetch(e, slot):
        return (pltpu.make_async_copy(win_ref.at[e], w1.at[slot], sems.at[0, slot]),
                pltpu.make_async_copy(wout_ref.at[e], w2.at[slot], sems.at[1, slot]))

    for copy in fetch(0, 0):
        copy.start()

    def per_expert(e, carry):
        slot = e % 2
        for copy in fetch(e, slot):
            copy.wait()

        @pl.when(e + 1 < experts)
        def _():
            for copy in fetch(e + 1, 1 - slot):
                copy.start()

        def per_peer(s, carry2):
            lo = bound_ref[s, e]
            hi = bound_ref[s, e + 1]
            first = lo // tile
            last = jnp.where(hi > lo, pl.cdiv(hi, tile), first)

            def per_tile(t, carry3):
                base = pl.multiple_of(t * tile, tile)
                x = x_ref[s, pl.ds(base, tile), :]
                for f in range(inner // cut):
                    pre = jnp.dot(x, w1[slot, :, f * cut:(f + 1) * cut], preferred_element_type=jnp.float32)
                    hidden[:, f * cut:(f + 1) * cut] = jax.nn.gelu(pre, approximate=True).astype(jnp.bfloat16)
                o = jnp.dot(hidden[...], w2[slot], preferred_element_type=jnp.float32)
                p = (gate_ref[s, pl.ds(base, tile), :] * o).astype(jnp.bfloat16).astype(jnp.float32)
                pos = base + lax.broadcasted_iota(jnp.int32, (tile, 1), 0)
                mine = (pos >= lo) & (pos < hi)
                old = out_ref[s, pl.ds(base, tile), :].astype(jnp.float32)
                out_ref[s, pl.ds(base, tile), :] = jnp.where(mine, p, old).astype(jnp.bfloat16)
                return carry3

            return lax.fori_loop(first, last, per_tile, carry2)

        return lax.fori_loop(0, peers, per_peer, carry)

    lax.fori_loop(0, experts, per_expert, 0)


def combine_kernel(ask_ref, live_ref, tok_ref, *refs):
    back_refs = refs[:CHUNKS]
    out_ref, raw, table, stage, rows_buf, out_buf, sems, row_sems, out_sems = refs[CHUNKS:]
    total, width = tok_ref.shape
    peers, block, _ = back_refs[0].shape
    mask = 2 * total - 1

    def fetch(c, d, slot):
        return pltpu.make_async_copy(back_refs[c].at[d], rows_buf.at[slot], row_sems.at[slot])

    fetch(0, 0, 0).start()
    load_table(tok_ref, raw, table, sems, total // sems.shape[0])
    for c in range(CHUNKS):

        def per_peer(d, carry, c=c):
            slot = (c * peers + d) % 2
            fetch(c, d, slot).wait()

            @pl.when(d + 1 < peers)
            def _():
                fetch(c, d + 1, 1 - slot).start()

            if c + 1 < CHUNKS:
                @pl.when(d + 1 == peers)
                def _():
                    fetch(c + 1, 0, 1 - slot).start()

            live = jnp.clip(live_ref[d] - c * block, 0, block)

            def group(g, carry2):
                base = pl.multiple_of(g * GROUP, GROUP)
                for k in range(width // LANES):
                    y = rows_buf[slot, pl.ds(base, GROUP), k * LANES:(k + 1) * LANES]
                    stage[pl.ds(k, GROUP, stride=SUB), :] = y.astype(jnp.float32)
                asks = [ask_ref[d, c * block + base + i] for i in range(GROUP)]
                spots = [pl.ds(pl.multiple_of((a & mask) * SUB, SUB), SUB) for a in asks]
                single = (asks[0] // (mask + 1)) == (asks[GROUP - 1] // (mask + 1))

                @pl.when(single)
                def _():
                    sums = [table[spots[i], :] + stage[i * SUB:(i + 1) * SUB, :] for i in range(GROUP)]
                    for i in range(GROUP):
                        table[spots[i], :] = sums[i]

                @pl.when(jnp.logical_not(single))
                def _():
                    for i in range(GROUP):
                        table[spots[i], :] = table[spots[i], :] + stage[i * SUB:(i + 1) * SUB, :]

                return carry2

            return lax.fori_loop(0, pl.cdiv(live, GROUP), group, carry)

        lax.fori_loop(0, peers, per_peer, 0)

    step = out_buf.shape[1]

    def flush(p, slot):
        return pltpu.make_async_copy(out_buf.at[slot], out_ref.at[pl.ds(p * step, step)], out_sems.at[slot])

    def write(p, carry):
        slot = p % 2

        @pl.when(p >= 2)
        def _():
            flush(p - 2, slot).wait()

        def convert(g, carry2):
            base = pl.multiple_of(g * GROUP, GROUP)
            for k in range(width // LANES):
                y = table[pl.ds((p * step + base) * SUB + k, GROUP, stride=SUB), :]
                out_buf[slot, pl.ds(base, GROUP), k * LANES:(k + 1) * LANES] = y.astype(jnp.bfloat16)
            return carry2

        lax.fori_loop(0, step // GROUP, convert, 0, unroll=2)
        flush(p, slot).start()
        return carry

    n_steps = total // step
    lax.fori_loop(0, n_steps, write, 0)
    for p in range(max(0, n_steps - 2), n_steps):
        flush(p, p % 2).wait()


def solution(mesh):
    peers = mesh.shape["ep"]
    row_spec = P(("dp", "ep"), None)
    expert_spec = P("ep", None, None)
    smem = pl.BlockSpec(memory_space=pltpu.SMEM)
    hbm = pl.BlockSpec(memory_space=pl.ANY)
    vmem = pl.BlockSpec(memory_space=pltpu.VMEM)
    params = pltpu.CompilerParams(vmem_limit_bytes=VMEM_LIMIT)

    def local_layer(tok, sel, gate, win, wout):
        rows, width = tok.shape
        experts, slots = sel.shape
        inner = win.shape[2]
        total = experts * slots
        cap = 2 * total // peers
        block = cap // CHUNKS
        parts = 8

        owner = sel // rows
        lane_e = lax.broadcasted_iota(jnp.int32, (experts, slots), 0)
        key = ((owner * (experts + 1) + lane_e) * rows + sel % rows).reshape(total)
        peer_ids = jnp.arange(peers, dtype=jnp.int32)
        counts = jnp.sum((owner.reshape(1, total) == peer_ids[:, None]).astype(jnp.int32), axis=1)
        fill_end = jnp.cumsum(cap - counts)
        fill_id = jnp.arange(peers * cap - total, dtype=jnp.int32)
        fill_owner = jnp.sum((fill_id[None, :] >= fill_end[:, None]).astype(jnp.int32), axis=0)
        fill_key = (fill_owner * (experts + 1) + experts) * rows + fill_id % rows
        keys, gates = lax.sort(
            (jnp.concatenate([key, fill_key]), jnp.concatenate([gate.reshape(total), jnp.zeros(fill_id.shape, jnp.float32)])),
            num_keys=1, is_stable=False)
        keys = keys.reshape(peers, cap)
        gates = gates.reshape(peers, cap)
        local = keys - peer_ids[:, None] * ((experts + 1) * rows)
        edges = jnp.arange(experts + 1, dtype=jnp.int32) * rows
        bounds = jnp.sum((local[:, None, :] < edges[None, :, None]).astype(jnp.int32), axis=2)
        which = local // rows
        want = which * (2 * rows) + jnp.where(which < experts, local % rows, rows)

        asked = lax.all_to_all(want, "ep", 0, 0, tiled=True)
        live = jnp.sum((asked < experts * 2 * rows).astype(jnp.int32), axis=1)

        def gather(c):
            return pl.pallas_call(
                functools.partial(gather_kernel, c),
                out_shape=jax.ShapeDtypeStruct((peers, block, width), jnp.bfloat16),
                in_specs=[smem, smem, hbm],
                out_specs=vmem,
                scratch_shapes=[
                    pltpu.VMEM((rows, width), jnp.bfloat16),
                    pltpu.VMEM(((rows + 1) * SUB, LANES), jnp.float32),
                    pltpu.VMEM((4 * GROUP * SUB, LANES), jnp.float32),
                    pltpu.SemaphoreType.DMA((parts,)),
                ],
                compiler_params=params,
                cost_estimate=pl.CostEstimate(flops=15_000_000_000, bytes_accessed=3 * rows * width, transcendentals=0),
                name="gather_rows",
            )(asked, live, tok)

        def ffn(c, x):
            cb = jnp.clip(bounds - c * block, 0, block)
            g = gates[:, c * block:(c + 1) * block].reshape(peers, block, 1)
            return pl.pallas_call(
                ffn_kernel,
                out_shape=jax.ShapeDtypeStruct((peers, block, width), jnp.bfloat16),
                in_specs=[smem, vmem, vmem, hbm, hbm],
                out_specs=vmem,
                scratch_shapes=[
                    pltpu.VMEM((2, width, inner), jnp.bfloat16),
                    pltpu.VMEM((2, inner, width), jnp.bfloat16),
                    pltpu.VMEM((min(ROW_TILE, block), inner), jnp.bfloat16),
                    pltpu.SemaphoreType.DMA((2, 2)),
                ],
                compiler_params=params,
                cost_estimate=pl.CostEstimate(
                    flops=4 * total * width * inner // CHUNKS, bytes_accessed=4 * experts * width * inner,
                    transcendentals=total * inner // CHUNKS),
                name="expert_ffn",
            )(cb, x, g, win, wout)

        arrived = [lax.all_to_all(gather(c), "ep", 0, 0, tiled=True) for c in range(CHUNKS)]
        back = [lax.all_to_all(ffn(c, arrived[c]), "ep", 0, 0, tiled=True) for c in range(CHUNKS)]

        step = rows // parts
        return pl.pallas_call(
            combine_kernel,
            out_shape=jax.ShapeDtypeStruct((rows, width), jnp.bfloat16),
            in_specs=[smem, smem, hbm] + [hbm] * CHUNKS,
            out_specs=hbm,
            scratch_shapes=[
                pltpu.VMEM((rows, width), jnp.bfloat16),
                pltpu.VMEM(((rows + 1) * SUB, LANES), jnp.float32),
                pltpu.VMEM((GROUP * SUB, LANES), jnp.float32),
                pltpu.VMEM((2, block, width), jnp.bfloat16),
                pltpu.VMEM((2, step, width), jnp.bfloat16),
                pltpu.SemaphoreType.DMA((parts,)),
                pltpu.SemaphoreType.DMA((2,)),
                pltpu.SemaphoreType.DMA((2,)),
            ],
            compiler_params=params,
            cost_estimate=pl.CostEstimate(flops=40_000_000_000, bytes_accessed=6 * rows * width, transcendentals=0),
            name="combine_rows",
        )(asked, live, tok, *back)

    return jax.shard_map(
        local_layer, mesh=mesh, in_specs=(row_spec, row_spec, row_spec, expert_spec, expert_spec),
        out_specs=row_spec, check_vma=False)
```

time: 1350 us -> 747 us (0.55)
  the two profiles are of different devices: /device:TPU:112 before, /device:TPU:119 now
where the time goes in v1:
time: 747 us; the launch traced here: 738 us
  Pallas kernels  328 us (44%)
  waiting for transfers between devices  252 us (34%)
  blocking collectives  85.1 us (11%)
  starting transfers between devices  52.3 us (7%)
  other arithmetic  9.98 us (1%)
  local copies, waits for them, and re-layouts  9.41 us (1%)
    all_to_all x4, waiting for transfers between devices, local_layer(): lax.all_to_all(gather(c), 'ep', 0, 0, tiled=True)  164 us
    pallas_call x4, Pallas kernels, ffn(): pl.pallas_call(ffn_kernel, out_shape=jax.ShapeDtypeStruct((peers, block,...  153 us
    pallas_call x1, Pallas kernels, local_layer(): pl.pallas_call(combine_kernel, out_shape=jax.ShapeDtypeStruct((rows, widt...  89.3 us
    all_to_all x3, waiting for transfers between devices, local_layer(): lax.all_to_all(ffn(c, arrived[c]), 'ep', 0, 0, tiled=True)  88.7 us
    pallas_call x4, Pallas kernels, gather(): pl.pallas_call(functools.partial(gather_kernel, c), out_shape=jax.ShapeDt...  85.7 us
    all_to_all x1, blocking collectives, local_layer(): lax.all_to_all(ffn(c, arrived[c]), 'ep', 0, 0, tiled=True)  77.3 us
    all_to_all x4, starting transfers between devices, local_layer(): lax.all_to_all(gather(c), 'ep', 0, 0, tiled=True)  29.6 us
    all_to_all x3, starting transfers between devices, local_layer(): lax.all_to_all(ffn(c, arrived[c]), 'ep', 0, 0, tiled=True)  22.7 us
  transfers between devices with their start and end apart: 7, of which 7 were waited for; matrix products, arithmetic and copies ran while one was open for 1% of the time, Pallas kernels for 30%

profile of v1, /device:TPU:119, one launch (start us, length us, event | category | flops | bytes accessed | tf_op | source)
XLA Modules:
  0.0 737.5 jit_solution(1256095213911979484)
XLA Ops:
  0.0 0.8 copy.37
  0.8 0.8 fusion.2
  1.6 0.2 convert_reduce_fusion.2
  1.8 0.2 reduce-window.8
  2.0 0.2 convert_reduce_fusion.1
  2.2 6.4 sort.15
  8.7 0.6 fusion
  9.3 7.8 %all_to_all.48 = s32[8,1,2048]{2,1,0:T(1,128)S(1)} all-to-all(s32[8,1,2048]{2,1,0:T(1,128)S(1)} %fusion), channel_id=1, replica_groups=mesh['dp'=2,'ep'=8] {'ep'}, dimensions={0} | all-to-all | bytes 131072 | tf_op jit(solution)/shard_map/all_to_all | solution.py:237
  17.1 0.6 convert_reduce_fusion.3.live_ref
  17.7 0.6 copy.41
  18.3 15.5 %gather_rows.7 = bf16[8,512,768]{2,1,0:T(8,128)(2,1)} custom-call(s32[8,2048]{1,0:T(8,128)} %bitcast.29, s32[8]{0:T(128)} %convert_reduce_fusion.3.live_ref, bf16[8192,768]{1,0:T(8,128)(2,1)} %tok_ref.9), custom_call_target="tpu_custom_call" | custom-call | flops 15000000512 | bytes 18874368 | tf_op jit(solution)/shard_map/gather_rows/pallas_call | solution.py:241
  33.9 6.4 all-to-all-start.7
  40.3 19.7 %gather_rows.6 = bf16[8,512,768]{2,1,0:T(8,128)(2,1)} custom-call(s32[8,2048]{1,0:T(8,128)} %bitcast.30, s32[8]{0:T(128)} %convert_reduce_fusion.3.live_ref, bf16[8192,768]{1,0:T(8,128)(2,1)} %tok_ref.9), custom_call_target="tpu_custom_call" | custom-call | flops 15000000512 | bytes 18874368 | tf_op jit(solution)/shard_map/gather_rows/pallas_call | solution.py:241
  60.0 49.1 %all-to-all-done.7.x_ref = bf16[8,512,768]{2,1,0:T(8,128)(2,1)} async-done(((bf16[8,512,768]{2,1,0:T(8,128)(2,1)}), bf16[8,512,768]{2,1,0:T(8,128)(2,1)}, u32[]{:S(2)}, u32[]{:S(2)}) %all-to-all-start.7) | async-done | bytes 6291488 | tf_op jit(solution)/shard_map/all_to_all | solution.py:278
  109.1 8.1 %all-to-all-start.5 = ((bf16[8,512,768]{2,1,0:T(8,128)(2,1)}), bf16[8,512,768]{2,1,0:T(8,128)(2,1)}, u32[]{:S(2)}, u32[]{:S(2)}) async-start(bf16[8,512,768]{2,1,0:T(8,128)(2,1)} %gather_rows.6), calls=%async_computation.5 | async-start | bytes 12582912 | tf_op jit(solution)/shard_map/all_to_all | solution.py:278
  117.2 24.6 %gather_rows.5 = bf16[8,512,768]{2,1,0:T(8,128)(2,1)} custom-call(s32[8,2048]{1,0:T(8,128)} %bitcast.31, s32[8]{0:T(128)} %convert_reduce_fusion.3.live_ref, bf16[8192,768]{1,0:T(8,128)(2,1)} %tok_ref.9), custom_call_target="tpu_custom_call" | custom-call | flops 15000000512 | bytes 18874368 | tf_op jit(solution)/shard_map/gather_rows/pallas_call | solution.py:241
  141.8 44.7 %all-to-all-done.5.x_ref = bf16[8,512,768]{2,1,0:T(8,128)(2,1)} async-done(((bf16[8,512,768]{2,1,0:T(8,128)(2,1)}), bf16[8,512,768]{2,1,0:T(8,128)(2,1)}, u32[]{:S(2)}, u32[]{:S(2)}) %all-to-all-start.5) | async-done | bytes 6291488 | tf_op jit(solution)/shard_map/all_to_all | solution.py:278
  186.5 7.5 %all-to-all-start.3 = ((bf16[8,512,768]{2,1,0:T(8,128)(2,1)}), bf16[8,512,768]{2,1,0:T(8,128)(2,1)}, u32[]{:S(2)}, u32[]{:S(2)}) async-start(bf16[8,512,768]{2,1,0:T(8,128)(2,1)} %gather_rows.5), calls=%async_computation.3 | async-start | bytes 12582912 | tf_op jit(solution)/shard_map/all_to_all | solution.py:278
  194.1 25.9 %gather_rows.4 = bf16[8,512,768]{2,1,0:T(8,128)(2,1)} custom-call(s32[8,2048]{1,0:T(8,128)} %bitcast.32, s32[8]{0:T(128)} %convert_reduce_fusion.3.live_ref, bf16[8192,768]{1,0:T(8,128)(2,1)} %tok_ref.9), custom_call_target="tpu_custom_call" | custom-call | flops 15000000512 | bytes 18874368 | tf_op jit(solution)/shard_map/gather_rows/pallas_call | solution.py:241
  220.0 43.4 %all-to-all-done.3.x_ref = bf16[8,512,768]{2,1,0:T(8,128)(2,1)} async-done(((bf16[8,512,768]{2,1,0:T(8,128)(2,1)}), bf16[8,512,768]{2,1,0:T(8,128)(2,1)}, u32[]{:S(2)}, u32[]{:S(2)}) %all-to-all-start.3) | async-done | bytes 6291488 | tf_op jit(solution)/shard_map/all_to_all | solution.py:278
  263.4 7.5 %all-to-all-start.1 = ((bf16[8,512,768]{2,1,0:T(8,128)(2,1)}), bf16[8,512,768]{2,1,0:T(8,128)(2,1)}, u32[]{:S(2)}, u32[]{:S(2)}) async-start(bf16[8,512,768]{2,1,0:T(8,128)(2,1)} %gather_rows.4), calls=%async_computation.1 | async-start | bytes 12582912 | tf_op jit(solution)/shard_map/all_to_all | solution.py:278
  270.9 0.1 broadcast_subtract_fusion
  271.0 0.3 convert_reduce_fusion
  271.3 0.1 copy.26
  271.4 2.0 copy.33.gate_ref
  273.4 0.6 add_clamp_fusion
  274.0 39.7 %expert_ffn.7 = bf16[8,512,768]{2,1,0:T(8,128)(2,1)} custom-call(s32[8,5]{1,0:T(8,128)} %get-tuple-element.15.bound_ref, bf16[8,512,768]{2,1,0:T(8,128)(2,1)} %all-to-all-done.7.x_ref, f32[8,512,1]{2,1,0:T(8,128)} %copy.33.gate_ref, bf16[4,768,3072]{2,1,0:T(8,128)(2,1)} %win_ref.7, bf16[4,3072,768]{2,1,0:T(8,128)(2,1)} %wout_ref.7), custom_call_target="tpu_custom_call" | custom-call | flops 19327352832 | bytes 37748736 | tf_op jit(solution)/shard_map/expert_ffn/pallas_call | solution.py:260
  313.6 26.6 %all-to-all-done.1.x_ref = bf16[8,512,768]{2,1,0:T(8,128)(2,1)} async-done(((bf16[8,512,768]{2,1,0:T(8,128)(2,1)}), bf16[8,512,768]{2,1,0:T(8,128)(2,1)}, u32[]{:S(2)}, u32[]{:S(2)}) %all-to-all-start.1) | async-done | bytes 6291488 | tf_op jit(solution)/shard_map/all_to_all | solution.py:278
  340.2 7.6 %all-to-all-start.8 = ((bf16[8,512,768]{2,1,0:T(8,128)(2,1)}), bf16[8,512,768]{2,1,0:T(8,128)(2,1)}, u32[]{:S(2)}, u32[]{:S(2)}) async-start(bf16[8,512,768]{2,1,0:T(8,128)(2,1)} %expert_ffn.7), calls=%async_computation.8 | async-start | bytes 12582912 | tf_op jit(solution)/shard_map/all_to_all | solution.py:279
  347.8 2.0 copy.31.gate_ref
  349.7 33.9 %expert_ffn.6 = bf16[8,512,768]{2,1,0:T(8,128)(2,1)} custom-call(s32[8,5]{1,0:T(8,128)} %get-tuple-element.16.bound_ref, bf16[8,512,768]{2,1,0:T(8,128)(2,1)} %all-to-all-done.5.x_ref, f32[8,512,1]{2,1,0:T(8,128)} %copy.31.gate_ref, bf16[4,768,3072]{2,1,0:T(8,128)(2,1)} %win_ref.7, bf16[4,3072,768]{2,1,0:T(8,128)(2,1)} %wout_ref.7), custom_call_target="tpu_custom_call" | custom-call | flops 19327352832 | bytes 37748736 | tf_op jit(solution)/shard_map/expert_ffn/pallas_call | solution.py:260
  383.6 33.5 %all-to-all-done.8.refs_3_ = bf16[8,512,768]{2,1,0:T(8,128)(2,1)} async-done(((bf16[8,512,768]{2,1,0:T(8,128)(2,1)}), bf16[8,512,768]{2,1,0:T(8,128)(2,1)}, u32[]{:S(2)}, u32[]{:S(2)}) %all-to-all-start.8) | async-done | bytes 6291488 | tf_op jit(solution)/shard_map/all_to_all | solution.py:279
  417.1 7.6 %all-to-all-start.6 = ((bf16[8,512,768]{2,1,0:T(8,128)(2,1)}), bf16[8,512,768]{2,1,0:T(8,128)(2,1)}, u32[]{:S(2)}, u32[]{:S(2)}) async-start(bf16[8,512,768]{2,1,0:T(8,128)(2,1)} %expert_ffn.6), calls=%async_computation.6 | async-start | bytes 12582912 | tf_op jit(solution)/shard_map/all_to_all | solution.py:279
  424.6 2.0 copy.29.gate_ref
  426.6 33.9 %expert_ffn.5 = bf16[8,512,768]{2,1,0:T(8,128)(2,1)} custom-call(s32[8,5]{1,0:T(8,128)} %get-tuple-element.17.bound_ref, bf16[8,512,768]{2,1,0:T(8,128)(2,1)} %all-to-all-done.3.x_ref, f32[8,512,1]{2,1,0:T(8,128)} %copy.29.gate_ref, bf16[4,768,3072]{2,1,0:T(8,128)(2,1)} %win_ref.7, bf16[4,3072,768]{2,1,0:T(8,128)(2,1)} %wout_ref.7), custom_call_target="tpu_custom_call" | custom-call | flops 19327352832 | bytes 37748736 | tf_op jit(solution)/shard_map/expert_ffn/pallas_call | solution.py:260
  460.5 33.4 %all-to-all-done.6.refs_2_ = bf16[8,512,768]{2,1,0:T(8,128)(2,1)} async-done(((bf16[8,512,768]{2,1,0:T(8,128)(2,1)}), bf16[8,512,768]{2,1,0:T(8,128)(2,1)}, u32[]{:S(2)}, u32[]{:S(2)}) %all-to-all-start.6) | async-done | bytes 6291488 | tf_op jit(solution)/shard_map/all_to_all | solution.py:279
  494.0 7.5 %all-to-all-start.4 = ((bf16[8,512,768]{2,1,0:T(8,128)(2,1)}), bf16[8,512,768]{2,1,0:T(8,128)(2,1)}, u32[]{:S(2)}, u32[]{:S(2)}) async-start(bf16[8,512,768]{2,1,0:T(8,128)(2,1)} %expert_ffn.5), calls=%async_computation.4 | async-start | bytes 12582912 | tf_op jit(solution)/shard_map/all_to_all | solution.py:279
  501.5 2.0 copy.27.gate_ref
  503.5 45.5 %expert_ffn.4 = bf16[8,512,768]{2,1,0:T(8,128)(2,1)} custom-call(s32[8,5]{1,0:T(8,128)} %get-tuple-element.18.bound_ref, bf16[8,512,768]{2,1,0:T(8,128)(2,1)} %all-to-all-done.1.x_ref, f32[8,512,1]{2,1,0:T(8,128)} %copy.27.gate_ref, bf16[4,768,3072]{2,1,0:T(8,128)(2,1)} %win_ref.7, bf16[4,3072,768]{2,1,0:T(8,128)(2,1)} %wout_ref.7), custom_call_target="tpu_custom_call" | custom-call | flops 19327352832 | bytes 37748736 | tf_op jit(solution)/shard_map/expert_ffn/pallas_call | solution.py:260
  549.0 21.8 %all-to-all-done.4.refs_1_ = bf16[8,512,768]{2,1,0:T(8,128)(2,1)} async-done(((bf16[8,512,768]{2,1,0:T(8,128)(2,1)}), bf16[8,512,768]{2,1,0:T(8,128)(2,1)}, u32[]{:S(2)}, u32[]{:S(2)}) %all-to-all-start.4) | async-done | bytes 6291488 | tf_op jit(solution)/shard_map/all_to_all | solution.py:279
  570.8 77.3 %all_to_all.49.refs_0_ = bf16[8,512,768]{2,1,0:T(8,128)(2,1)} all-to-all(bf16[8,512,768]{2,1,0:T(8,128)(2,1)} %expert_ffn.4), channel_id=1, replica_groups=mesh['dp'=2,'ep'=8] {'ep'}, dimensions={0} | all-to-all | bytes 12582912 | tf_op jit(solution)/shard_map/all_to_all | solution.py:279
  648.1 89.3 %combine_rows.1 = bf16[8192,768]{1,0:T(8,128)(2,1)} custom-call(s32[8,2048]{1,0:T(8,128)} %bitcast.33, s32[8]{0:T(128)} %convert_reduce_fusion.3.live_ref, bf16[8192,768]{1,0:T(8,128)(2,1)} %tok_ref.9, bf16[8,512,768]{2,1,0:T(8,128)(2,1)} %all_to_all.49.refs_0_, bf16[8,512,768]{2,1,0:T(8,128)(2,1)} %all-to-all-done.4.refs_1_, ...), custom_call_target="tpu_custom_call" | custom-call | flops 40000000000 | bytes 37748736 | tf_op jit(solution)/shard_map/combine_rows/pallas_call | solution.py:282
  (11 shorter events, 0.1 us)
Async XLA Ops:
  33.9 75.2 %all-to-all-start.7 = ((bf16[8,512,768]{2,1,0:T(8,128)(2,1)}), bf16[8,512,768]{2,1,0:T(8,128)(2,1)}, u32[]{:S(2)}, u32[]{:S(2)}) async-start(bf16[8,512,768]{2,1,0:T(8,128)(2,1)} %gather_rows.7), calls=%async_computation.7 | async-start | bytes 12582912 | tf_op jit(solution)/shard_map/all_to_all | solution.py:278
  109.1 77.4 %all-to-all-start.5 = ((bf16[8,512,768]{2,1,0:T(8,128)(2,1)}), bf16[8,512,768]{2,1,0:T(8,128)(2,1)}, u32[]{:S(2)}, u32[]{:S(2)}) async-start(bf16[8,512,768]{2,1,0:T(8,128)(2,1)} %gather_rows.6), calls=%async_computation.5 | async-start | bytes 12582912 | tf_op jit(solution)/shard_map/all_to_all | solution.py:278
  186.5 76.8 %all-to-all-start.3 = ((bf16[8,512,768]{2,1,0:T(8,128)(2,1)}), bf16[8,512,768]{2,1,0:T(8,128)(2,1)}, u32[]{:S(2)}, u32[]{:S(2)}) async-start(bf16[8,512,768]{2,1,0:T(8,128)(2,1)} %gather_rows.5), calls=%async_computation.3 | async-start | bytes 12582912 | tf_op jit(solution)/shard_map/all_to_all | solution.py:278
  263.4 76.8 %all-to-all-start.1 = ((bf16[8,512,768]{2,1,0:T(8,128)(2,1)}), bf16[8,512,768]{2,1,0:T(8,128)(2,1)}, u32[]{:S(2)}, u32[]{:S(2)}) async-start(bf16[8,512,768]{2,1,0:T(8,128)(2,1)} %gather_rows.4), calls=%async_computation.1 | async-start | bytes 12582912 | tf_op jit(solution)/shard_map/all_to_all | solution.py:278
  340.2 76.9 %all-to-all-start.8 = ((bf16[8,512,768]{2,1,0:T(8,128)(2,1)}), bf16[8,512,768]{2,1,0:T(8,128)(2,1)}, u32[]{:S(2)}, u32[]{:S(2)}) async-start(bf16[8,512,768]{2,1,0:T(8,128)(2,1)} %expert_ffn.7), calls=%async_computation.8 | async-start | bytes 12582912 | tf_op jit(solution)/shard_map/all_to_all | solution.py:279
  417.1 76.9 %all-to-all-start.6 = ((bf16[8,512,768]{2,1,0:T(8,128)(2,1)}), bf16[8,512,768]{2,1,0:T(8,128)(2,1)}, u32[]{:S(2)}, u32[]{:S(2)}) async-start(bf16[8,512,768]{2,1,0:T(8,128)(2,1)} %expert_ffn.6), calls=%async_computation.6 | async-start | bytes 12582912 | tf_op jit(solution)/shard_map/all_to_all | solution.py:279
  494.0 76.8 %all-to-all-start.4 = ((bf16[8,512,768]{2,1,0:T(8,128)(2,1)}), bf16[8,512,768]{2,1,0:T(8,128)(2,1)}, u32[]{:S(2)}, u32[]{:S(2)}) async-start(bf16[8,512,768]{2,1,0:T(8,128)(2,1)} %expert_ffn.5), calls=%async_computation.4 | async-start | bytes 12582912 | tf_op jit(solution)/shard_map/all_to_all | solution.py:279

commit v2 on v1

--- a/solution.py
+++ b/solution.py
@@ -11,7 +11,8 @@
 SUB = 8
 GROUP = 16
 VMEM_LIMIT = 62 * 1024 * 1024
-CHUNKS = 4
+PAIR = 2 * GROUP
+SHARES = (5, 3)
 ROW_TILE = 256
 
 
@@ -37,34 +38,38 @@
         lax.fori_loop(0, rows // GROUP, convert, 0, unroll=2)
 
 
-def gather_kernel(chunk, ask_ref, live_ref, tok_ref, out_ref, raw, table, stage, sems):
+def gather_kernel(start, cap, ask_ref, live_ref, tok_ref, out_ref, raw, table, stage, sems):
     total, width = tok_ref.shape
     peers, block, _ = out_ref.shape
     load_table(tok_ref, raw, table, sems, total // sems.shape[0])
     mask = 2 * total - 1
 
     def per_peer(d, carry):
-        live = jnp.clip(live_ref[d] - chunk * block, 0, block)
+        live = jnp.clip(live_ref[d] - start, 0, block)
 
         def group(g, carry2):
-            base = pl.multiple_of(g * GROUP, GROUP)
-            slot = pl.multiple_of((g % 4) * GROUP * SUB, GROUP * SUB)
-            for i in range(GROUP):
-                row = ask_ref[d, chunk * block + base + i] & mask
+            base = pl.multiple_of(g * PAIR, PAIR)
+            first = d * cap + start + base
+            slot = pl.multiple_of((g % 2) * PAIR * SUB, PAIR * SUB)
+            for i in range(PAIR):
+                row = ask_ref[first + i]
+                if i % GROUP == 0:
+                    row = row & mask
                 stage[pl.ds(slot + i * SUB, SUB), :] = table[pl.ds(pl.multiple_of(row * SUB, SUB), SUB), :]
-            for k in range(width // LANES):
-                y = stage[pl.ds(slot + k, GROUP, stride=SUB), :]
-                out_ref[d, pl.ds(base, GROUP), k * LANES:(k + 1) * LANES] = y.astype(jnp.bfloat16)
+            for h in range(PAIR // GROUP):
+                for k in range(width // LANES):
+                    y = stage[pl.ds(slot + h * GROUP * SUB + k, GROUP, stride=SUB), :]
+                    out_ref[d, pl.ds(base + h * GROUP, GROUP), k * LANES:(k + 1) * LANES] = y.astype(jnp.bfloat16)
             return carry2
 
-        return lax.fori_loop(0, pl.cdiv(live, GROUP), group, carry)
+        return lax.fori_loop(0, pl.cdiv(live, PAIR), group, carry)
 
     lax.fori_loop(0, peers, per_peer, 0)
 
 
 def ffn_kernel(bound_ref, x_ref, gate_ref, win_ref, wout_ref, out_ref, w1, w2, hidden, sems):
-    experts, width, inner = win_ref.shape
-    peers, block, _ = x_ref.shape
+    experts, _, inner = win_ref.shape
+    peers, _, _ = x_ref.shape
     tile = hidden.shape[0]
     cut = 512
 
@@ -112,61 +117,87 @@
     lax.fori_loop(0, experts, per_expert, 0)
 
 
-def combine_kernel(ask_ref, live_ref, tok_ref, *refs):
-    back_refs = refs[:CHUNKS]
-    out_ref, raw, table, stage, rows_buf, out_buf, sems, row_sems, out_sems = refs[CHUNKS:]
-    total, width = tok_ref.shape
-    peers, block, _ = back_refs[0].shape
-    mask = 2 * total - 1
-
-    def fetch(c, d, slot):
-        return pltpu.make_async_copy(back_refs[c].at[d], rows_buf.at[slot], row_sems.at[slot])
-
-    fetch(0, 0, 0).start()
+def add_rows(start, cap, ask_ref, live_ref, back_ref, table, stage, rows_buf, row_sems, mask):
+    peers, block, width = back_ref.shape
+
+    def fetch(d, slot):
+        return pltpu.make_async_copy(back_ref.at[d], rows_buf.at[slot], row_sems.at[slot])
+
+    def per_peer(d, carry):
+        slot = d % 2
+        fetch(d, slot).wait()
+
+        @pl.when(d + 1 < peers)
+        def _():
+            fetch(d + 1, 1 - slot).start()
+
+        live = jnp.clip(live_ref[d] - start, 0, block)
+
+        def group(g, carry2):
+            base = pl.multiple_of(g * PAIR, PAIR)
+            for h in range(PAIR // GROUP):
+                for k in range(width // LANES):
+                    y = rows_buf[slot, pl.ds(base + h * GROUP, GROUP), k * LANES:(k + 1) * LANES]
+                    stage[pl.ds(h * GROUP * SUB + k, GROUP, stride=SUB), :] = y.astype(jnp.float32)
+            first = d * cap + start + base
+            asks = [ask_ref[first + i] for i in range(PAIR)]
+            mixed = asks[0] > mask
+            for h in range(1, PAIR // GROUP):
+                mixed = jnp.logical_or(mixed, asks[h * GROUP] > mask)
+            spots = [pl.ds(pl.multiple_of(((a & mask) if i % GROUP == 0 else a) * SUB, SUB), SUB)
+                     for i, a in enumerate(asks)]
+
+            @pl.when(jnp.logical_not(mixed))
+            def _():
+                for h in range(PAIR // GROUP):
+                    ids = range(h * GROUP, (h + 1) * GROUP)
+                    sums = [table[spots[i], :] + stage[i * SUB:(i + 1) * SUB, :] for i in ids]
+                    for i, v in zip(ids, sums):
+                        table[spots[i], :] = v
+
+            @pl.when(mixed)
+            def _():
+                for i in range(PAIR):
+                    table[spots[i], :] = table[spots[i], :] + stage[i * SUB:(i + 1) * SUB, :]
+
+            return carry2
+
+        return lax.fori_loop(0, pl.cdiv(live, PAIR), group, carry)
+
+    return fetch, lambda: lax.fori_loop(0, peers, per_peer, 0)
+
+
+def first_combine_kernel(start, cap, ask_ref, live_ref, tok_ref, back_ref, sum_ref, raw, table, stage, rows_buf,
+                         sems, row_sems, sum_sems):
+    total, _ = tok_ref.shape
+    fetch, run = add_rows(start, cap, ask_ref, live_ref, back_ref, table, stage, rows_buf, row_sems, 2 * total - 1)
+    fetch(0, 0).start()
     load_table(tok_ref, raw, table, sems, total // sems.shape[0])
-    for c in range(CHUNKS):
-
-        def per_peer(d, carry, c=c):
-            slot = (c * peers + d) % 2
-            fetch(c, d, slot).wait()
-
-            @pl.when(d + 1 < peers)
-            def _():
-                fetch(c, d + 1, 1 - slot).start()
-
-            if c + 1 < CHUNKS:
-                @pl.when(d + 1 == peers)
-                def _():
-                    fetch(c + 1, 0, 1 - slot).start()
-
-            live = jnp.clip(live_ref[d] - c * block, 0, block)
-
-            def group(g, carry2):
-                base = pl.multiple_of(g * GROUP, GROUP)
-                for k in range(width // LANES):
-                    y = rows_buf[slot, pl.ds(base, GROUP), k * LANES:(k + 1) * LANES]
-                    stage[pl.ds(k, GROUP, stride=SUB), :] = y.astype(jnp.float32)
-                asks = [ask_ref[d, c * block + base + i] for i in range(GROUP)]
-                spots = [pl.ds(pl.multiple_of((a & mask) * SUB, SUB), SUB) for a in asks]
-                single = (asks[0] // (mask + 1)) == (asks[GROUP - 1] // (mask + 1))
-
-                @pl.when(single)
-                def _():
-                    sums = [table[spots[i], :] + stage[i * SUB:(i + 1) * SUB, :] for i in range(GROUP)]
-                    for i in range(GROUP):
-                        table[spots[i], :] = sums[i]
-
-                @pl.when(jnp.logical_not(single))
-                def _():
-                    for i in range(GROUP):
-                        table[spots[i], :] = table[spots[i], :] + stage[i * SUB:(i + 1) * SUB, :]
-
-                return carry2
-
-            return lax.fori_loop(0, pl.cdiv(live, GROUP), group, carry)
-
-        lax.fori_loop(0, peers, per_peer, 0)
-
+    run()
+    parts = sum_sems.shape[0]
+    step = total * SUB // parts
+    copies = [pltpu.make_async_copy(table.at[pl.ds(p * step, step)], sum_ref.at[pl.ds(p * step, step)], sum_sems.at[p])
+              for p in range(parts)]
+    for copy in copies:
+        copy.start()
+    for copy in copies:
+        copy.wait()
+
+
+def last_combine_kernel(start, cap, ask_ref, live_ref, sum_ref, back_ref, out_ref, table, stage, rows_buf, out_buf,
+                        row_sems, sum_sems, out_sems):
+    total, width = out_ref.shape
+    fetch, run = add_rows(start, cap, ask_ref, live_ref, back_ref, table, stage, rows_buf, row_sems, 2 * total - 1)
+    parts = sum_sems.shape[0]
+    part = total * SUB // parts
+    copies = [pltpu.make_async_copy(sum_ref.at[pl.ds(p * part, part)], table.at[pl.ds(p * part, part)], sum_sems.at[p])
+              for p in range(parts)]
+    for copy in copies:
+        copy.start()
+    fetch(0, 0).start()
+    for copy in copies:
+        copy.wait()
+    run()
     step = out_buf.shape[1]
 
     def flush(p, slot):
@@ -211,8 +242,10 @@
         inner = win.shape[2]
         total = experts * slots
         cap = 2 * total // peers
-        block = cap // CHUNKS
         parts = 8
+        chunks = []
+        for share in SHARES:
+            chunks.append((sum(n for _, n in chunks), share * cap // 8))
 
         owner = sel // rows
         lane_e = lax.broadcasted_iota(jnp.int32, (experts, slots), 0)
@@ -232,21 +265,25 @@
         edges = jnp.arange(experts + 1, dtype=jnp.int32) * rows
         bounds = jnp.sum((local[:, None, :] < edges[None, :, None]).astype(jnp.int32), axis=2)
         which = local // rows
-        want = which * (2 * rows) + jnp.where(which < experts, local % rows, rows)
+        lane = lax.broadcasted_iota(jnp.int32, (peers, cap), 1)
+        mixed = (lane % GROUP == 0) & (which != jnp.roll(which, 1 - GROUP, axis=1))
+        want = jnp.where(which < experts, local % rows, rows) + jnp.where(mixed, 2 * rows, 0)
 
         asked = lax.all_to_all(want, "ep", 0, 0, tiled=True)
-        live = jnp.sum((asked < experts * 2 * rows).astype(jnp.int32), axis=1)
+        live = jnp.sum((asked & (2 * rows - 1) != rows).astype(jnp.int32), axis=1)
+        asked = asked.reshape(peers * cap)
 
         def gather(c):
+            start, block = chunks[c]
             return pl.pallas_call(
-                functools.partial(gather_kernel, c),
+                functools.partial(gather_kernel, start, cap),
                 out_shape=jax.ShapeDtypeStruct((peers, block, width), jnp.bfloat16),
                 in_specs=[smem, smem, hbm],
                 out_specs=vmem,
                 scratch_shapes=[
                     pltpu.VMEM((rows, width), jnp.bfloat16),
                     pltpu.VMEM(((rows + 1) * SUB, LANES), jnp.float32),
-                    pltpu.VMEM((4 * GROUP * SUB, LANES), jnp.float32),
+                    pltpu.VMEM((2 * PAIR * SUB, LANES), jnp.float32),
                     pltpu.SemaphoreType.DMA((parts,)),
                 ],
                 compiler_params=params,
@@ -255,8 +292,9 @@
             )(asked, live, tok)
 
         def ffn(c, x):
-            cb = jnp.clip(bounds - c * block, 0, block)
-            g = gates[:, c * block:(c + 1) * block].reshape(peers, block, 1)
+            start, block = chunks[c]
+            cb = jnp.clip(bounds - start, 0, block)
+            g = gates[:, start:start + block].reshape(peers, block, 1)
             return pl.pallas_call(
                 ffn_kernel,
                 out_shape=jax.ShapeDtypeStruct((peers, block, width), jnp.bfloat16),
@@ -270,34 +308,53 @@
                 ],
                 compiler_params=params,
                 cost_estimate=pl.CostEstimate(
-                    flops=4 * total * width * inner // CHUNKS, bytes_accessed=4 * experts * width * inner,
-                    transcendentals=total * inner // CHUNKS),
+                    flops=4 * total * width * inner // len(chunks), bytes_accessed=4 * experts * width * inner,
+                    transcendentals=total * inner // len(chunks)),
                 name="expert_ffn",
             )(cb, x, g, win, wout)
 
-        arrived = [lax.all_to_all(gather(c), "ep", 0, 0, tiled=True) for c in range(CHUNKS)]
-        back = [lax.all_to_all(ffn(c, arrived[c]), "ep", 0, 0, tiled=True) for c in range(CHUNKS)]
+        def exchange(x):
+            return lax.all_to_all(x, "ep", 0, 0, tiled=True)
+
+        sent = [gather(c) for c in range(2)]
+        in_a = exchange(sent[0])
+        in_b = exchange(sent[1])
+        done_a = ffn(0, in_a)
+        done_b = ffn(1, in_b)
+        back_a = exchange(done_a)
+        back_b = exchange(done_b)
 
         step = rows // parts
-        return pl.pallas_call(
-            combine_kernel,
-            out_shape=jax.ShapeDtypeStruct((rows, width), jnp.bfloat16),
-            in_specs=[smem, smem, hbm] + [hbm] * CHUNKS,
+        table_shape = pltpu.VMEM(((rows + 1) * SUB, LANES), jnp.float32)
+        stage_shape = pltpu.VMEM((PAIR * SUB, LANES), jnp.float32)
+        two = pltpu.SemaphoreType.DMA((2,))
+        sums = pl.pallas_call(
+            functools.partial(first_combine_kernel, chunks[0][0], cap),
+            out_shape=jax.ShapeDtypeStruct((rows * SUB, LANES), jnp.float32),
+            in_specs=[smem, smem, hbm, hbm],
             out_specs=hbm,
             scratch_shapes=[
-                pltpu.VMEM((rows, width), jnp.bfloat16),
-                pltpu.VMEM(((rows + 1) * SUB, LANES), jnp.float32),
-                pltpu.VMEM((GROUP * SUB, LANES), jnp.float32),
-                pltpu.VMEM((2, block, width), jnp.bfloat16),
-                pltpu.VMEM((2, step, width), jnp.bfloat16),
-                pltpu.SemaphoreType.DMA((parts,)),
-                pltpu.SemaphoreType.DMA((2,)),
-                pltpu.SemaphoreType.DMA((2,)),
+                pltpu.VMEM((rows, width), jnp.bfloat16), table_shape, stage_shape,
+                pltpu.VMEM((2, chunks[0][1], width), jnp.bfloat16),
+                pltpu.SemaphoreType.DMA((parts,)), two, pltpu.SemaphoreType.DMA((parts,)),
             ],
             compiler_params=params,
             cost_estimate=pl.CostEstimate(flops=40_000_000_000, bytes_accessed=6 * rows * width, transcendentals=0),
-            name="combine_rows",
-        )(asked, live, tok, *back)
+            name="combine_first",
+        )(asked, live, tok, back_a)
+        return pl.pallas_call(
+            functools.partial(last_combine_kernel, chunks[1][0], cap),
+            out_shape=jax.ShapeDtypeStruct((rows, width), jnp.bfloat16),
+            in_specs=[smem, smem, hbm, hbm],
+            out_specs=hbm,
+            scratch_shapes=[
+                table_shape, stage_shape, pltpu.VMEM((2, chunks[1][1], width), jnp.bfloat16),
+                pltpu.VMEM((2, step, width), jnp.bfloat16), two, pltpu.SemaphoreType.DMA((parts,)), two,
+            ],
+            compiler_params=params,
+            cost_estimate=pl.CostEstimate(flops=20_000_000_000, bytes_accessed=6 * rows * width, transcendentals=0),
+            name="combine_last",
+        )(asked, live, sums, back_b)
 
     return jax.shard_map(
         local_layer, mesh=mesh, in_specs=(row_spec, row_spec, row_spec, expert_spec, expert_spec),

time: 747 us -> 669 us (0.90)
  the two profiles are of different devices: /device:TPU:119 before, /device:TPU:112 now
where the time goes in v2:
time: 669 us; the launch traced here: 665 us
  waiting for transfers between devices  359 us (54%)
  Pallas kernels  248 us (37%)
  starting transfers between devices  30.9 us (5%)
  blocking collectives  10.7 us (2%)
  other arithmetic  9.66 us (1%)
    all_to_all x4, waiting for transfers between devices, exchange(): return lax.all_to_all(x, 'ep', 0, 0, tiled=True)  359 us
    pallas_call x2, Pallas kernels, ffn(): pl.pallas_call(ffn_kernel, out_shape=jax.ShapeDtypeStruct((peers, block,...  138 us
    pallas_call x1, Pallas kernels, local_layer(): pl.pallas_call(functools.partial(first_combine_kernel, chunks[0][0], cap)...  40.2 us
    pallas_call x2, Pallas kernels, gather(): pl.pallas_call(functools.partial(gather_kernel, start, cap), out_shape=ja...  36.4 us
    pallas_call x1, Pallas kernels, local_layer(): pl.pallas_call(functools.partial(last_combine_kernel, chunks[1][0], cap),...  33.5 us
    all_to_all x4, starting transfers between devices, exchange(): return lax.all_to_all(x, 'ep', 0, 0, tiled=True)  30.9 us
  transfers between devices with their start and end apart: 4, of which 4 were waited for; matrix products, arithmetic and copies ran while one was open for 1% of the time, Pallas kernels for 29%

profile of v2, /device:TPU:112, one launch (start us, length us, event | category | flops | bytes accessed | tf_op | source)
XLA Modules:
  0.0 664.8 jit_solution(11889192575169521515)
XLA Ops:
  0.0 0.8 fusion.8
  0.8 0.2 convert_reduce_fusion.2
  1.0 0.2 reduce-window.8
  1.2 0.2 convert_reduce_fusion.1
  1.4 0.8 copy.22
  2.2 6.4 sort.15
  8.7 0.1 add_select_fusion
  8.8 0.1 slice_bitcast_fusion
  8.9 0.1 fusion.1
  9.1 0.1 copy.14
  9.1 10.7 %all_to_all.26 = s32[8,1,2048]{2,1,0:T(1,128)S(1)} all-to-all(s32[8,1,2048]{2,1,0:T(1,128)S(1)} %copy.14), channel_id=1, replica_groups=mesh['dp'=2,'ep'=8] {'ep'}, dimensions={0} | all-to-all | bytes 131072 | tf_op jit(solution)/shard_map/all_to_all | solution.py:272
  19.9 0.0 copy-start
  19.9 0.7 convert_reduce_fusion.3.live_ref
  20.6 0.0 copy-done
  20.6 21.5 %gather_rows.2 = bf16[8,1280,768]{2,1,0:T(8,128)(2,1)} custom-call(s32[16384]{0:T(1024)} %bitcast.20, s32[8]{0:T(128)} %convert_reduce_fusion.3.live_ref, bf16[8192,768]{1,0:T(8,128)(2,1)} %tok_ref.5), custom_call_target="tpu_custom_call" | custom-call | flops 15000000512 | bytes 18874368 | tf_op jit(solution)/shard_map/gather_rows/pallas_call | solution.py:278
  42.1 10.5 %all-to-all-start.1 = ((bf16[8,1280,768]{2,1,0:T(8,128)(2,1)}), bf16[8,1280,768]{2,1,0:T(8,128)(2,1)}, u32[]{:S(2)}, u32[]{:S(2)}) async-start(bf16[8,1280,768]{2,1,0:T(8,128)(2,1)} %gather_rows.2), calls=%async_computation.1 | async-start | bytes 31457280 | tf_op jit(solution)/shard_map/all_to_all | solution.py:317
  52.6 14.9 %gather_rows.3 = bf16[8,768,768]{2,1,0:T(8,128)(2,1)} custom-call(s32[16384]{0:T(1024)} %bitcast.21, s32[8]{0:T(128)} %convert_reduce_fusion.3.live_ref, bf16[8192,768]{1,0:T(8,128)(2,1)} %tok_ref.5), custom_call_target="tpu_custom_call" | custom-call | flops 15000000512 | bytes 18874368 | tf_op jit(solution)/shard_map/gather_rows/pallas_call | solution.py:278
  67.4 158.5 %all-to-all-done.1.x_ref = bf16[8,1280,768]{2,1,0:T(8,128)(2,1)} async-done(((bf16[8,1280,768]{2,1,0:T(8,128)(2,1)}), bf16[8,1280,768]{2,1,0:T(8,128)(2,1)}, u32[]{:S(2)}, u32[]{:S(2)}) %all-to-all-start.1) | async-done | bytes 15728672 | tf_op jit(solution)/shard_map/all_to_all | solution.py:317
  225.9 5.2 all-to-all-start.3
  231.2 0.3 convert_reduce_fusion
  231.5 0.1 copy.16
  231.6 3.1 copy.17.gate_ref
  234.7 0.6 add_clamp_fusion
  235.3 101.1 %expert_ffn.2 = bf16[8,1280,768]{2,1,0:T(8,128)(2,1)} custom-call(s32[8,5]{1,0:T(8,128)} %get-tuple-element.14.bound_ref, bf16[8,1280,768]{2,1,0:T(8,128)(2,1)} %all-to-all-done.1.x_ref, f32[8,1280,1]{2,1,0:T(8,128)} %copy.17.gate_ref, bf16[4,768,3072]{2,1,0:T(8,128)(2,1)} %win_ref.3, bf16[4,3072,768]{2,1,0:T(8,128)(2,1)} %wout_ref.3), custom_call_target="tpu_custom_call" | custom-call | flops 38654705664 | bytes 37748736 | tf_op jit(solution)/shard_map/expert_ffn/pallas_call | solution.py:298
  336.4 0.4 all-to-all-done.3.x_ref
  336.9 10.0 %all-to-all-start.2 = ((bf16[8,1280,768]{2,1,0:T(8,128)(2,1)}), bf16[8,1280,768]{2,1,0:T(8,128)(2,1)}, u32[]{:S(2)}, u32[]{:S(2)}) async-start(bf16[8,1280,768]{2,1,0:T(8,128)(2,1)} %expert_ffn.2), calls=%async_computation.2 | async-start | bytes 31457280 | tf_op jit(solution)/shard_map/all_to_all | solution.py:317
  346.9 2.2 copy.19.gate_ref
  349.1 36.7 %expert_ffn.3 = bf16[8,768,768]{2,1,0:T(8,128)(2,1)} custom-call(s32[8,5]{1,0:T(8,128)} %get-tuple-element.13.bound_ref, bf16[8,768,768]{2,1,0:T(8,128)(2,1)} %all-to-all-done.3.x_ref, f32[8,768,1]{2,1,0:T(8,128)} %copy.19.gate_ref, bf16[4,768,3072]{2,1,0:T(8,128)(2,1)} %win_ref.3, bf16[4,3072,768]{2,1,0:T(8,128)(2,1)} %wout_ref.3), custom_call_target="tpu_custom_call" | custom-call | flops 38654705664 | bytes 37748736 | tf_op jit(solution)/shard_map/expert_ffn/pallas_call | solution.py:298
  385.8 134.5 %all-to-all-done.2.back_ref = bf16[8,1280,768]{2,1,0:T(8,128)(2,1)} async-done(((bf16[8,1280,768]{2,1,0:T(8,128)(2,1)}), bf16[8,1280,768]{2,1,0:T(8,128)(2,1)}, u32[]{:S(2)}, u32[]{:S(2)}) %all-to-all-start.2) | async-done | bytes 15728672 | tf_op jit(solution)/shard_map/all_to_all | solution.py:317
  520.2 5.2 all-to-all-start.4
  525.5 40.2 %combine_first.1.sum_ref = f32[65536,128]{1,0:T(8,128)} custom-call(s32[16384]{0:T(1024)} %bitcast.22, s32[8]{0:T(128)} %convert_reduce_fusion.3.live_ref, bf16[8192,768]{1,0:T(8,128)(2,1)} %tok_ref.5, bf16[8,1280,768]{2,1,0:T(8,128)(2,1)} %all-to-all-done.2.back_ref), custom_call_target="tpu_custom_call" | custom-call | flops 40000000000 | bytes 37748736 | tf_op jit(solution)/shard_map/combine_first/pallas_call | solution.py:331
  565.7 65.5 %all-to-all-done.4.back_ref = bf16[8,768,768]{2,1,0:T(8,128)(2,1)} async-done(((bf16[8,768,768]{2,1,0:T(8,128)(2,1)}), bf16[8,768,768]{2,1,0:T(8,128)(2,1)}, u32[]{:S(2)}, u32[]{:S(2)}) %all-to-all-start.4) | async-done | bytes 9437216 | tf_op jit(solution)/shard_map/all_to_all | solution.py:317
  631.2 33.5 %combine_last.1 = bf16[8192,768]{1,0:T(8,128)(2,1)} custom-call(s32[16384]{0:T(1024)} %bitcast.23, s32[8]{0:T(128)} %convert_reduce_fusion.3.live_ref, f32[65536,128]{1,0:T(8,128)} %combine_first.1.sum_ref, bf16[8,768,768]{2,1,0:T(8,128)(2,1)} %all-to-all-done.4.back_ref), custom_call_target="tpu_custom_call" | custom-call | flops 20000000000 | bytes 37748736 | tf_op jit(solution)/shard_map/combine_last/pallas_call | solution.py:345
  (16 shorter events, 0.1 us)
Async XLA Ops:
  19.9 0.7 copy-start
  42.1 183.9 %all-to-all-start.1 = ((bf16[8,1280,768]{2,1,0:T(8,128)(2,1)}), bf16[8,1280,768]{2,1,0:T(8,128)(2,1)}, u32[]{:S(2)}, u32[]{:S(2)}) async-start(bf16[8,1280,768]{2,1,0:T(8,128)(2,1)} %gather_rows.2), calls=%async_computation.1 | async-start | bytes 31457280 | tf_op jit(solution)/shard_map/all_to_all | solution.py:317
  225.9 111.0 %all-to-all-start.3 = ((bf16[8,768,768]{2,1,0:T(8,128)(2,1)}), bf16[8,768,768]{2,1,0:T(8,128)(2,1)}, u32[]{:S(2)}, u32[]{:S(2)}) async-start(bf16[8,768,768]{2,1,0:T(8,128)(2,1)} %gather_rows.3), calls=%async_computation.3 | async-start | bytes 18874368 | tf_op jit(solution)/shard_map/all_to_all | solution.py:317
  336.9 183.3 %all-to-all-start.2 = ((bf16[8,1280,768]{2,1,0:T(8,128)(2,1)}), bf16[8,1280,768]{2,1,0:T(8,128)(2,1)}, u32[]{:S(2)}, u32[]{:S(2)}) async-start(bf16[8,1280,768]{2,1,0:T(8,128)(2,1)} %expert_ffn.2), calls=%async_computation.2 | async-start | bytes 31457280 | tf_op jit(solution)/shard_map/all_to_all | solution.py:317
  520.2 111.0 %all-to-all-start.4 = ((bf16[8,768,768]{2,1,0:T(8,128)(2,1)}), bf16[8,768,768]{2,1,0:T(8,128)(2,1)}, u32[]{:S(2)}, u32[]{:S(2)}) async-start(bf16[8,768,768]{2,1,0:T(8,128)(2,1)} %expert_ffn.3), calls=%async_computation.4 | async-start | bytes 18874368 | tf_op jit(solution)/shard_map/all_to_all | solution.py:317

commit v3 on v2

--- a/solution.py
+++ b/solution.py
@@ -38,16 +38,25 @@
         lax.fori_loop(0, rows // GROUP, convert, 0, unroll=2)
 
 
-def gather_kernel(start, cap, ask_ref, live_ref, tok_ref, out_ref, raw, table, stage, sems):
+def gather_kernel(start, cap, dest_ref, ask_ref, live_ref, tok_ref, *refs):
     total, width = tok_ref.shape
-    peers, block, _ = out_ref.shape
+    peers = dest_ref.shape[0]
+    out_refs = refs[:peers]
+    raw, table, stage, out_buf, sems, out_sems = refs[peers:]
+    block = out_refs[0].shape[0]
     load_table(tok_ref, raw, table, sems, total // sems.shape[0])
     mask = 2 * total - 1
 
-    def per_peer(d, carry):
+    def flush(j):
+        return pltpu.make_async_copy(out_buf.at[j % 2], out_refs[j], out_sems.at[j % 2])
+
+    for j in range(peers):
+        if j >= 2:
+            flush(j - 2).wait()
+        d = dest_ref[j]
         live = jnp.clip(live_ref[d] - start, 0, block)
 
-        def group(g, carry2):
+        def group(g, carry, j=j, d=d):
             base = pl.multiple_of(g * PAIR, PAIR)
             first = d * cap + start + base
             slot = pl.multiple_of((g % 2) * PAIR * SUB, PAIR * SUB)
@@ -59,17 +68,20 @@
             for h in range(PAIR // GROUP):
                 for k in range(width // LANES):
                     y = stage[pl.ds(slot + h * GROUP * SUB + k, GROUP, stride=SUB), :]
-                    out_ref[d, pl.ds(base + h * GROUP, GROUP), k * LANES:(k + 1) * LANES] = y.astype(jnp.bfloat16)
-            return carry2
-
-        return lax.fori_loop(0, pl.cdiv(live, PAIR), group, carry)
-
-    lax.fori_loop(0, peers, per_peer, 0)
-
-
-def ffn_kernel(bound_ref, x_ref, gate_ref, win_ref, wout_ref, out_ref, w1, w2, hidden, sems):
+                    out_buf[j % 2, pl.ds(base + h * GROUP, GROUP), k * LANES:(k + 1) * LANES] = y.astype(jnp.bfloat16)
+            return carry
+
+        lax.fori_loop(0, pl.cdiv(live, PAIR), group, 0)
+        flush(j).start()
+    for j in range(peers - 2, peers):
+        flush(j).wait()
+
+
+def ffn_kernel(bound_ref, gate_ref, win_ref, wout_ref, *refs):
     experts, _, inner = win_ref.shape
-    peers, _, _ = x_ref.shape
+    peers = bound_ref.shape[0]
+    x_refs, out_refs = refs[:peers], refs[peers:2 * peers]
+    xs, outs, w1, w2, hidden, sems, x_sems, out_sems = refs[2 * peers:]
     tile = hidden.shape[0]
     cut = 512
 
@@ -77,8 +89,17 @@
         return (pltpu.make_async_copy(win_ref.at[e], w1.at[slot], sems.at[0, slot]),
                 pltpu.make_async_copy(wout_ref.at[e], w2.at[slot], sems.at[1, slot]))
 
+    def bring(s):
+        return pltpu.make_async_copy(x_refs[s], xs.at[s], x_sems.at[s])
+
+    def flush(s):
+        return pltpu.make_async_copy(outs.at[s], out_refs[s], out_sems.at[s])
+
+    bring(0).start()
     for copy in fetch(0, 0):
         copy.start()
+    for s in range(1, peers):
+        bring(s).start()
 
     def per_expert(e, carry):
         slot = e % 2
@@ -91,6 +112,10 @@
                 copy.start()
 
         def per_peer(s, carry2):
+            @pl.when(e == 0)
+            def _():
+                pltpu.make_async_copy(x_refs[0], xs.at[s], x_sems.at[s]).wait()
+
             lo = bound_ref[s, e]
             hi = bound_ref[s, e + 1]
             first = lo // tile
@@ -98,7 +123,7 @@
 
             def per_tile(t, carry3):
                 base = pl.multiple_of(t * tile, tile)
-                x = x_ref[s, pl.ds(base, tile), :]
+                x = xs[s, pl.ds(base, tile), :]
                 for f in range(inner // cut):
                     pre = jnp.dot(x, w1[slot, :, f * cut:(f + 1) * cut], preferred_element_type=jnp.float32)
                     hidden[:, f * cut:(f + 1) * cut] = jax.nn.gelu(pre, approximate=True).astype(jnp.bfloat16)
@@ -106,31 +131,41 @@
                 p = (gate_ref[s, pl.ds(base, tile), :] * o).astype(jnp.bfloat16).astype(jnp.float32)
                 pos = base + lax.broadcasted_iota(jnp.int32, (tile, 1), 0)
                 mine = (pos >= lo) & (pos < hi)
-                old = out_ref[s, pl.ds(base, tile), :].astype(jnp.float32)
-                out_ref[s, pl.ds(base, tile), :] = jnp.where(mine, p, old).astype(jnp.bfloat16)
+                old = outs[s, pl.ds(base, tile), :].astype(jnp.float32)
+                outs[s, pl.ds(base, tile), :] = jnp.where(mine, p, old).astype(jnp.bfloat16)
                 return carry3
 
-            return lax.fori_loop(first, last, per_tile, carry2)
+            lax.fori_loop(first, last, per_tile, 0)
+            for j in range(peers):
+                @pl.when((e == experts - 1) & (s == j))
+                def _():
+                    flush(j).start()
+
+            return carry2
 
         return lax.fori_loop(0, peers, per_peer, carry)
 
     lax.fori_loop(0, experts, per_expert, 0)
-
-
-def add_rows(start, cap, ask_ref, live_ref, back_ref, table, stage, rows_buf, row_sems, mask):
-    peers, block, width = back_ref.shape
-
-    def fetch(d, slot):
-        return pltpu.make_async_copy(back_ref.at[d], rows_buf.at[slot], row_sems.at[slot])
-
-    def per_peer(d, carry):
-        slot = d % 2
-        fetch(d, slot).wait()
-
-        @pl.when(d + 1 < peers)
-        def _():
-            fetch(d + 1, 1 - slot).start()
-
+    for s in range(peers):
+        flush(s).wait()
+
+
+def add_rows(start, cap, dest_ref, ask_ref, live_ref, back_refs, table, stage, rows_buf, row_sems, mask):
+    peers = len(back_refs)
+    block, width = back_refs[0].shape
+
+    def fetch(j, slot):
+        return pltpu.make_async_copy(back_refs[j], rows_buf.at[slot], row_sems.at[slot])
+
+    def per_peer(j, carry):
+        slot = j % 2
+        fetch(0, slot).wait()
+        for n in range(1, peers):
+            @pl.when(j + 1 == n)
+            def _():
+                fetch(n, 1 - slot).start()
+
+        d = dest_ref[j]
         live = jnp.clip(live_ref[d] - start, 0, block)
 
         def group(g, carry2):
@@ -167,10 +202,12 @@
     return fetch, lambda: lax.fori_loop(0, peers, per_peer, 0)
 
 
-def first_combine_kernel(start, cap, ask_ref, live_ref, tok_ref, back_ref, sum_ref, raw, table, stage, rows_buf,
-                         sems, row_sems, sum_sems):
+def first_combine_kernel(start, cap, dest_ref, ask_ref, live_ref, tok_ref, *refs):
     total, _ = tok_ref.shape
-    fetch, run = add_rows(start, cap, ask_ref, live_ref, back_ref, table, stage, rows_buf, row_sems, 2 * total - 1)
+    peers = dest_ref.shape[0]
+    back_refs = refs[:peers]
+    sum_ref, raw, table, stage, rows_buf, sems, row_sems, sum_sems = refs[peers:]
+    fetch, run = add_rows(start, cap, dest_ref, ask_ref, live_ref, back_refs, table, stage, rows_buf, row_sems, 2 * total - 1)
     fetch(0, 0).start()
     load_table(tok_ref, raw, table, sems, total // sems.shape[0])
     run()
@@ -184,10 +221,12 @@
         copy.wait()
 
 
-def last_combine_kernel(start, cap, ask_ref, live_ref, sum_ref, back_ref, out_ref, table, stage, rows_buf, out_buf,
-                        row_sems, sum_sems, out_sems):
+def last_combine_kernel(start, cap, dest_ref, ask_ref, live_ref, sum_ref, *refs):
+    peers = dest_ref.shape[0]
+    back_refs = refs[:peers]
+    out_ref, table, stage, rows_buf, out_buf, row_sems, sum_sems, out_sems = refs[peers:]
     total, width = out_ref.shape
-    fetch, run = add_rows(start, cap, ask_ref, live_ref, back_ref, table, stage, rows_buf, row_sems, 2 * total - 1)
+    fetch, run = add_rows(start, cap, dest_ref, ask_ref, live_ref, back_refs, table, stage, rows_buf, row_sems, 2 * total - 1)
     parts = sum_sems.shape[0]
     part = total * SUB // parts
     copies = [pltpu.make_async_copy(sum_ref.at[pl.ds(p * part, part)], table.at[pl.ds(p * part, part)], sum_sems.at[p])
@@ -229,6 +268,7 @@
 
 def solution(mesh):
     peers = mesh.shape["ep"]
+    chips = peers // 2
     row_spec = P(("dp", "ep"), None)
     expert_spec = P("ep", None, None)
     smem = pl.BlockSpec(memory_space=pltpu.SMEM)
@@ -273,56 +313,80 @@
         live = jnp.sum((asked & (2 * rows - 1) != rows).astype(jnp.int32), axis=1)
         asked = asked.reshape(peers * cap)
 
+        hops = [(0, 0), (1, 0), (1, 1), (chips - 1, 0), (chips - 1, 1), (0, 1)]
+        hops += [(n, flip) for n in range(2, chips - 1) for flip in (0, 1)]
+        me = lax.axis_index("ep")
+        dests = jnp.stack([(me // 2 + n) % chips * 2 + (me % 2 + f) % 2 for n, f in hops])
+        sources = jnp.stack([(me // 2 + chips - n) % chips * 2 + (me % 2 + f) % 2 for n, f in hops])
+        onehot = (sources[:, None] == peer_ids[None, :]).astype(jnp.int32)
+
+        def exchange(xs, forward):
+            ys = []
+            for x, (n, f) in zip(xs, hops):
+                there = [(i // 2 + n) % chips * 2 + (i % 2 + f) % 2 for i in range(peers)]
+                pairs = [(i, j) if forward else (j, i) for i, j in enumerate(there)]
+                ys.append(x if (n, f) == (0, 0) else lax.ppermute(x, "ep", pairs))
+            return ys
+
+        def blocks(c):
+            return [jax.ShapeDtypeStruct((chunks[c][1], width), jnp.bfloat16)] * peers
+
         def gather(c):
             start, block = chunks[c]
             return pl.pallas_call(
                 functools.partial(gather_kernel, start, cap),
-                out_shape=jax.ShapeDtypeStruct((peers, block, width), jnp.bfloat16),
-                in_specs=[smem, smem, hbm],
-                out_specs=vmem,
+                out_shape=blocks(c),
+                in_specs=[smem, smem, smem, hbm],
+                out_specs=[hbm] * peers,
                 scratch_shapes=[
                     pltpu.VMEM((rows, width), jnp.bfloat16),
                     pltpu.VMEM(((rows + 1) * SUB, LANES), jnp.float32),
                     pltpu.VMEM((2 * PAIR * SUB, LANES), jnp.float32),
+                    pltpu.VMEM((2, block, width), jnp.bfloat16),
                     pltpu.SemaphoreType.DMA((parts,)),
+                    pltpu.SemaphoreType.DMA((2,)),
                 ],
                 compiler_params=params,
                 cost_estimate=pl.CostEstimate(flops=15_000_000_000, bytes_accessed=3 * rows * width, transcendentals=0),
                 name="gather_rows",
-            )(asked, live, tok)
+            )(dests, asked, live, tok)
 
         def ffn(c, x):
             start, block = chunks[c]
-            cb = jnp.clip(bounds - start, 0, block)
-            g = gates[:, start:start + block].reshape(peers, block, 1)
+            cb = jnp.clip(hop_bounds - start, 0, block)
+            g = hop_gates[:, start:start + block].reshape(peers, block, 1)
             return pl.pallas_call(
                 ffn_kernel,
-                out_shape=jax.ShapeDtypeStruct((peers, block, width), jnp.bfloat16),
-                in_specs=[smem, vmem, vmem, hbm, hbm],
-                out_specs=vmem,
+                out_shape=blocks(c),
+                in_specs=[smem, vmem, hbm, hbm] + [hbm] * peers,
+                out_specs=[hbm] * peers,
                 scratch_shapes=[
+                    pltpu.VMEM((peers, block, width), jnp.bfloat16),
+                    pltpu.VMEM((peers, block, width), jnp.bfloat16),
                     pltpu.VMEM((2, width, inner), jnp.bfloat16),
                     pltpu.VMEM((2, inner, width), jnp.bfloat16),
                     pltpu.VMEM((min(ROW_TILE, block), inner), jnp.bfloat16),
                     pltpu.SemaphoreType.DMA((2, 2)),
+                    pltpu.SemaphoreType.DMA((peers,)),
+                    pltpu.SemaphoreType.DMA((peers,)),
                 ],
                 compiler_params=params,
                 cost_estimate=pl.CostEstimate(
                     flops=4 * total * width * inner // len(chunks), bytes_accessed=4 * experts * width * inner,
                     transcendentals=total * inner // len(chunks)),
                 name="expert_ffn",
-            )(cb, x, g, win, wout)
-
-        def exchange(x):
-            return lax.all_to_all(x, "ep", 0, 0, tiled=True)
+            )(cb, g, win, wout, *x)
+
+        hop_bounds = jnp.sum(onehot[:, :, None] * bounds[None], axis=1)
+        hop_gates = jnp.sum(jnp.where(onehot[:, :, None] > 0, gates[None], 0.0), axis=1)
 
         sent = [gather(c) for c in range(2)]
-        in_a = exchange(sent[0])
-        in_b = exchange(sent[1])
+        in_a = exchange(sent[0], True)
+        in_b = exchange(sent[1], True)
         done_a = ffn(0, in_a)
         done_b = ffn(1, in_b)
-        back_a = exchange(done_a)
-        back_b = exchange(done_b)
+        back_a = exchange(done_a, False)
+        back_b = exchange(done_b, False)
 
         step = rows // parts
         table_shape = pltpu.VMEM(((rows + 1) * SUB, LANES), jnp.float32)
@@ -331,7 +395,7 @@
         sums = pl.pallas_call(
             functools.partial(first_combine_kernel, chunks[0][0], cap),
             out_shape=jax.ShapeDtypeStruct((rows * SUB, LANES), jnp.float32),
-            in_specs=[smem, smem, hbm, hbm],
+            in_specs=[smem, smem, smem, hbm] + [hbm] * peers,
             out_specs=hbm,
             scratch_shapes=[
                 pltpu.VMEM((rows, width), jnp.bfloat16), table_shape, stage_shape,
@@ -341,11 +405,11 @@
             compiler_params=params,
             cost_estimate=pl.CostEstimate(flops=40_000_000_000, bytes_accessed=6 * rows * width, transcendentals=0),
             name="combine_first",
-        )(asked, live, tok, back_a)
+        )(dests, asked, live, tok, *back_a)
         return pl.pallas_call(
             functools.partial(last_combine_kernel, chunks[1][0], cap),
             out_shape=jax.ShapeDtypeStruct((rows, width), jnp.bfloat16),
-            in_specs=[smem, smem, hbm, hbm],
+            in_specs=[smem, smem, smem, hbm] + [hbm] * peers,
             out_specs=hbm,
             scratch_shapes=[
                 table_shape, stage_shape, pltpu.VMEM((2, chunks[1][1], width), jnp.bfloat16),
@@ -354,7 +418,7 @@
             compiler_params=params,
             cost_estimate=pl.CostEstimate(flops=20_000_000_000, bytes_accessed=6 * rows * width, transcendentals=0),
             name="combine_last",
-        )(asked, live, sums, back_b)
+        )(dests, asked, live, sums, *back_b)
 
     return jax.shard_map(
         local_layer, mesh=mesh, in_specs=(row_spec, row_spec, row_spec, expert_spec, expert_spec),

time: 669 us -> 776 us (1.16)
  starting transfers between devices: 30.9 us -> 240 us
  waiting for transfers between devices: 359 us -> 277 us
  Pallas kernels: 248 us -> 237 us
  blocking collectives: 10.7 us -> 0 us
    all_to_all x4 -> x1, waiting for transfers between devices: 359 us -> 4.96 us  [local_layer(): asked = lax.all_to_all(want, 'ep', 0, 0, tiled=True)]
    ppermute x0 -> x28, waiting for transfers between devices: none -> 272 us  [exchange(): ys.append(x if (n, f) == (0, 0) else lax.ppermute(x, 'ep', pairs))]
    ppermute x0 -> x28, starting transfers between devices: none -> 235 us  [exchange(): ys.append(x if (n, f) == (0, 0) else lax.ppermute(x, 'ep', pairs))]
    all_to_all x4 -> x1, starting transfers between devices: 30.9 us -> 5.3 us  [local_layer(): asked = lax.all_to_all(want, 'ep', 0, 0, tiled=True)]
    all_to_all x1 -> x0, blocking collectives: 10.7 us -> none  [local_layer(): asked = lax.all_to_all(want, 'ep', 0, 0, tiled=True)]
    pallas_call x4, Pallas kernels: 174 us -> 166 us  [the longest x2 131 us: ffn(): pl.pallas_call(ffn_kernel, out_shape=blocks(c), in_specs=[smem, vmem, hbm...]
  transfers between devices with their start and end apart: 4 -> 29, of which waited for: 4 -> 10; matrix products, arithmetic and copies ran while one was open for 1% -> 1% of each run, Pallas kernels for 29% -> 24%
where the time goes in v3:
time: 776 us; the launch traced here: 773 us
  waiting for transfers between devices  277 us (36%)
  starting transfers between devices  240 us (31%)
  Pallas kernels  237 us (31%)
  other arithmetic  10.1 us (1%)
  local copies, waits for them, and re-layouts  7.84 us (1%)
    ppermute x28, waiting for transfers between devices, exchange(): ys.append(x if (n, f) == (0, 0) else lax.ppermute(x, 'ep', pairs))  272 us
    ppermute x28, starting transfers between devices, exchange(): ys.append(x if (n, f) == (0, 0) else lax.ppermute(x, 'ep', pairs))  235 us
    pallas_call x2, Pallas kernels, ffn(): pl.pallas_call(ffn_kernel, out_shape=blocks(c), in_specs=[smem, vmem, hbm...  131 us
    pallas_call x1, Pallas kernels, local_layer(): pl.pallas_call(functools.partial(first_combine_kernel, chunks[0][0], cap)...  38.8 us
    pallas_call x2, Pallas kernels, gather(): pl.pallas_call(functools.partial(gather_kernel, start, cap), out_shape=bl...  34.7 us
    pallas_call x1, Pallas kernels, local_layer(): pl.pallas_call(functools.partial(last_combine_kernel, chunks[1][0], cap),...  32.3 us
  transfers between devices with their start and end apart: 29, of which 10 were waited for; matrix products, arithmetic and copies ran while one was open for 1% of the time, Pallas kernels for 24%

profile of v3, /device:TPU:112, one launch (start us, length us, event | category | flops | bytes accessed | tf_op | source)
XLA Modules:
  0.0 773.1 jit_solution(14027355037950751799)
XLA Ops:
  0.0 0.8 fusion.8
  0.8 0.2 convert_reduce_fusion.2
  1.0 0.2 reduce-window.8
  1.2 0.2 convert_reduce_fusion.1
  1.4 0.8 copy.22
  2.2 6.4 sort.15
  8.7 0.1 add_select_fusion
  8.8 0.1 slice_bitcast_fusion
  8.9 0.1 fusion.1
  9.1 0.7 copy.14
  9.8 5.3 all-to-all-start
  15.1 0.7 stack.50.dest_ref
  15.7 5.0 all-to-all-done
  20.7 0.7 convert_reduce_fusion.3.live_ref
  21.4 19.6 %gather_rows.2 = (bf16[1280,768]{1,0:T(8,128)(2,1)}, bf16[1280,768]{1,0:T(8,128)(2,1)}, bf16[1280,768]{1,0:T(8,128)(2,1)}, bf16[1280,768]{1,0:T(8,128)(2,1)}, bf...) custom-call(s32[8]{0:T(128)} %stack.50.dest_ref, ...), custom_call_target="tpu_custom_call" | custom-call | flops 15000000512 | bytes 18874368 | tf_op jit(solution)/shard_map/gather_rows/pallas_call | solution.py:336
  41.0 4.2 collective-permute-start
  45.3 0.5 collective-permute-start.1
  45.7 15.0 %gather_rows.3 = (bf16[768,768]{1,0:T(8,128)(2,1)}, bf16[768,768]{1,0:T(8,128)(2,1)}, bf16[768,768]{1,0:T(8,128)(2,1)}, bf16[768,768]{1,0:T(8,128)(2,1)}, bf16[7...) custom-call(s32[8]{0:T(128)} %stack.50.dest_ref, ...), custom_call_target="tpu_custom_call" | custom-call | flops 15000000512 | bytes 18874368 | tf_op jit(solution)/shard_map/gather_rows/pallas_call | solution.py:336
  60.8 2.4 collective-permute-start.14
  63.2 0.9 collective-permute-start.15
  64.1 2.7 collective-permute-start.2
  66.8 89.4 %collective-permute-done.14.refs_1_ = bf16[768,768]{1,0:T(8,128)(2,1)S(1)} collective-permute-done((bf16[768,768]{1,0:T(8,128)(2,1)}, bf16[768,768]{1,0:T(8,128)(2,1)S(1)}, u32[]{:S(2)}, u32[]{:S(2)}) %collective-permute-start.14) | collective-permute-done | bytes 1179680 | tf_op jit(solution)/shard_map/ppermute | solution.py:328
  156.2 1.2 collective-permute-start.3
  157.4 23.6 %collective-permute-done.15.refs_2_ = bf16[768,768]{1,0:T(8,128)(2,1)} collective-permute-done((bf16[768,768]{1,0:T(8,128)(2,1)}, bf16[768,768]{1,0:T(8,128)(2,1)}, u32[]{:S(2)}, u32[]{:S(2)}) %collective-permute-start.15) | collective-permute-done | bytes 1179680 | tf_op jit(solution)/shard_map/ppermute | solution.py:328
  181.0 3.3 collective-permute-start.5
  184.3 0.1 collective-permute-start.6
  184.4 0.1 stack.53
  184.5 0.3 convert_reduce_fusion
  184.7 0.1 broadcast_compare_fusion.1
  184.8 0.2 multiply_reduce_fusion
  185.0 0.1 copy.16
  185.1 0.2 select_reduce_fusion
  185.3 3.2 copy.17.gate_ref
  188.5 2.2 copy.19.gate_ref
  190.7 0.6 add_clamp_fusion
  191.3 0.0 collective-permute-done.2.refs_3_
  191.3 2.5 collective-permute-start.16
  193.9 5.9 collective-permute-done.3.refs_4_
  199.8 5.4 collective-permute-start.17
  205.2 0.0 collective-permute-done.4.refs_5_
  205.2 86.3 %collective-permute-start.18 = (bf16[768,768]{1,0:T(8,128)(2,1)}, bf16[768,768]{1,0:T(8,128)(2,1)}, u32[]{:S(2)}, u32[]{:S(2)}) collective-permute-start(bf16[768,768]{1,0:T(8,128)(2,1)} %get-tuple-element.62), channel_id=1, source_target_pairs={{0,1},{1,0},{2,3},{3,2},{4,5},{5,4},{6,7},{7,6},{8,9},{9,8},{10,11... | collective-permute-start | bytes 3538952 | tf_op jit(solution)/shard_map/ppermute | solution.py:328
  291.5 2.9 collective-permute-start.20
  294.5 97.1 %expert_ffn.2 = (bf16[1280,768]{1,0:T(8,128)(2,1)}, bf16[1280,768]{1,0:T(8,128)(2,1)}, bf16[1280,768]{1,0:T(8,128)(2,1)}, bf16[1280,768]{1,0:T(8,128)(2,1)}, bf1...) custom-call(s32[8,5]{1,0:T(8,128)} %get-tuple-element.78.bound_ref, ...), custom_call_target="tpu_custom_call" | custom-call | flops 38654705664 | bytes 37748736 | tf_op jit(solution)/shard_map/expert_ffn/pallas_call | solution.py:358
  391.5 0.0 collective-permute-done.16.refs_3_
  391.5 0.0 copy-start.3
  391.5 0.1 collective-permute-start.7
  391.7 0.0 collective-permute-done.17.refs_4_
  391.7 0.9 collective-permute-start.8
  392.6 34.3 %expert_ffn.3 = (bf16[768,768]{1,0:T(8,128)(2,1)}, bf16[768,768]{1,0:T(8,128)(2,1)}, bf16[768,768]{1,0:T(8,128)(2,1)}, bf16[768,768]{1,0:T(8,128)(2,1)}, bf16[76...) custom-call(s32[8,5]{1,0:T(8,128)} %get-tuple-element.77.bound_ref, ...), custom_call_target="tpu_custom_call" | custom-call | flops 38654705664 | bytes 37748736 | tf_op jit(solution)/shard_map/expert_ffn/pallas_call | solution.py:358
  426.9 19.5 %collective-permute-start.21 = (bf16[768,768]{1,0:T(8,128)(2,1)}, bf16[768,768]{1,0:T(8,128)(2,1)S(1)}, u32[]{:S(2)}, u32[]{:S(2)}) collective-permute-start(bf16[768,768]{1,0:T(8,128)(2,1)} %get-tuple-element.66), channel_id=1, source_target_pairs={{2,0},{3,1},{4,2},{5,3},{6,4},{7,5},{0,6},{1,7},{10,8},{11,9},{12,... | collective-permute-start | bytes 3538952 | tf_op jit(solution)/shard_map/ppermute | solution.py:328
  446.4 55.2 %collective-permute-done.21.refs_1_ = bf16[768,768]{1,0:T(8,128)(2,1)S(1)} collective-permute-done((bf16[768,768]{1,0:T(8,128)(2,1)}, bf16[768,768]{1,0:T(8,128)(2,1)S(1)}, u32[]{:S(2)}, u32[]{:S(2)}) %collective-permute-start.21) | collective-permute-done | bytes 1179680 | tf_op jit(solution)/shard_map/ppermute | solution.py:328
  501.6 6.1 collective-permute-start.10
  507.7 22.7 %collective-permute-done.22.refs_2_ = bf16[768,768]{1,0:T(8,128)(2,1)} collective-permute-done((bf16[768,768]{1,0:T(8,128)(2,1)}, bf16[768,768]{1,0:T(8,128)(2,1)}, u32[]{:S(2)}, u32[]{:S(2)}) %collective-permute-start.22) | collective-permute-done | bytes 1179680 | tf_op jit(solution)/shard_map/ppermute | solution.py:328
  530.3 0.1 collective-permute-start.12
  530.5 3.2 collective-permute-start.13
  533.7 16.9 %collective-permute-done.10.refs_4_ = bf16[1280,768]{1,0:T(8,128)(2,1)} collective-permute-done((bf16[1280,768]{1,0:T(8,128)(2,1)}, bf16[1280,768]{1,0:T(8,128)(2,1)}, u32[]{:S(2)}, u32[]{:S(2)}) %collective-permute-start.10) | collective-permute-done | bytes 1966112 | tf_op jit(solution)/shard_map/ppermute | solution.py:328
  550.6 89.2 %collective-permute-start.24 = (bf16[768,768]{1,0:T(8,128)(2,1)}, bf16[768,768]{1,0:T(8,128)(2,1)}, u32[]{:S(2)}, u32[]{:S(2)}) collective-permute-start(bf16[768,768]{1,0:T(8,128)(2,1)} %get-tuple-element.69), channel_id=1, source_target_pairs={{7,0},{6,1},{1,2},{0,3},{3,4},{2,5},{5,6},{4,7},{15,8},{14,9},{9,1... | collective-permute-start | bytes 3538952 | tf_op jit(solution)/shard_map/ppermute | solution.py:328
  639.8 3.0 collective-permute-start.26
  642.9 0.3 collective-permute-start.27
  643.2 38.8 %combine_first.1.sum_ref = f32[65536,128]{1,0:T(8,128)} custom-call(s32[8]{0:T(128)} %stack.50.dest_ref, s32[16384]{0:T(1024)} %bitcast.32, s32[8]{0:T(128)} %convert_reduce_fusion.3.live_ref, bf16[8192,768]{1,0:T(8,128)(2,1)} %tok_ref.5, bf16[1280,768]{1,0:T(8,128)(2,1)} %get-tuple-element.49.refs_0_, bf16[1280,768]{1,0:T(8,128)(2,1)} %collective-permute-done.7.refs_1_, ...), custom_call_target="tpu_custom_call" | custom-call | flops 40000000000 | bytes 37748736 | tf_op jit(solution)/shard_map/combine_first/pallas_call | solution.py:395
  682.1 3.4 collective-permute-done.24.refs_4_
  685.5 31.7 %collective-permute-done.26.refs_6_ = bf16[768,768]{1,0:T(8,128)(2,1)} collective-permute-done((bf16[768,768]{1,0:T(8,128)(2,1)}, bf16[768,768]{1,0:T(8,128)(2,1)}, u32[]{:S(2)}, u32[]{:S(2)}) %collective-permute-start.26) | collective-permute-done | bytes 1179680 | tf_op jit(solution)/shard_map/ppermute | solution.py:328
  717.2 23.4 %collective-permute-done.27.refs_7_ = bf16[768,768]{1,0:T(8,128)(2,1)} collective-permute-done((bf16[768,768]{1,0:T(8,128)(2,1)}, bf16[768,768]{1,0:T(8,128)(2,1)}, u32[]{:S(2)}, u32[]{:S(2)}) %collective-permute-start.27) | collective-permute-done | bytes 1179680 | tf_op jit(solution)/shard_map/ppermute | solution.py:328
  740.6 32.3 %combine_last.1 = bf16[8192,768]{1,0:T(8,128)(2,1)} custom-call(s32[8]{0:T(128)} %stack.50.dest_ref, s32[16384]{0:T(1024)} %bitcast.33, s32[8]{0:T(128)} %convert_reduce_fusion.3.live_ref, f32[65536,128]{1,0:T(8,128)} %combine_first.1.sum_ref, bf16[768,768]{1,0:T(8,128)(2,1)} %get-tuple-element.65.refs_0_, bf16[768,768]{1,0:T(8,128)(2,1)} %copy-done.2, ...), custom_call_target="tpu_custom_call" | custom-call | flops 20000000000 | bytes 37748736 | tf_op jit(solution)/shard_map/combine_last/pallas_call | solution.py:409
  (45 shorter events, 0.2 us)
Async XLA Ops:
  9.8 10.9 %all-to-all-start = ((s32[8,1,2048]{2,1,0:T(1,128)}), s32[8,1,2048]{2,1,0:T(1,128)S(1)}, u32[]{:S(2)}, u32[]{:S(2)}) async-start(s32[8,1,2048]{2,1,0:T(1,128)} %copy.14), calls=%async_computation | async-start | bytes 131072 | tf_op jit(solution)/shard_map/all_to_all | solution.py:312
  20.7 0.7 copy-start
  41.0 140.0 %collective-permute-start = (bf16[1280,768]{1,0:T(8,128)(2,1)}, bf16[1280,768]{1,0:T(8,128)(2,1)}, u32[]{:S(2)}, u32[]{:S(2)}) collective-permute-start(bf16[1280,768]{1,0:T(8,128)(2,1)} %get-tuple-element.42), channel_id=1, source_target_pairs={{0,2},{1,3},{2,4},{3,5},{4,6},{5,7},{6,0},{7,1},{8,10},{9,11},{10,... | collective-permute-start | bytes 5898248 | tf_op jit(solution)/shard_map/ppermute | solution.py:328
  45.3 139.0 %collective-permute-start.1 = (bf16[1280,768]{1,0:T(8,128)(2,1)}, bf16[1280,768]{1,0:T(8,128)(2,1)}, u32[]{:S(2)}, u32[]{:S(2)}) collective-permute-start(bf16[1280,768]{1,0:T(8,128)(2,1)} %get-tuple-element.43), channel_id=1, source_target_pairs={{0,3},{1,2},{2,5},{3,4},{4,7},{5,6},{6,1},{7,0},{8,11},{9,10},{10,... | collective-permute-start | bytes 5898248 | tf_op jit(solution)/shard_map/ppermute | solution.py:328
  60.8 95.4 %collective-permute-start.14 = (bf16[768,768]{1,0:T(8,128)(2,1)}, bf16[768,768]{1,0:T(8,128)(2,1)S(1)}, u32[]{:S(2)}, u32[]{:S(2)}) collective-permute-start(bf16[768,768]{1,0:T(8,128)(2,1)} %get-tuple-element.58), channel_id=1, source_target_pairs={{0,2},{1,3},{2,4},{3,5},{4,6},{5,7},{6,0},{7,1},{8,10},{9,11},{10,... | collective-permute-start | bytes 3538952 | tf_op jit(solution)/shard_map/ppermute | solution.py:328
  63.2 117.8 %collective-permute-start.15 = (bf16[768,768]{1,0:T(8,128)(2,1)}, bf16[768,768]{1,0:T(8,128)(2,1)}, u32[]{:S(2)}, u32[]{:S(2)}) collective-permute-start(bf16[768,768]{1,0:T(8,128)(2,1)} %get-tuple-element.59), channel_id=1, source_target_pairs={{0,3},{1,2},{2,5},{3,4},{4,7},{5,6},{6,1},{7,0},{8,11},{9,10},{10,... | collective-permute-start | bytes 3538952 | tf_op jit(solution)/shard_map/ppermute | solution.py:328
  64.1 127.2 %collective-permute-start.2 = (bf16[1280,768]{1,0:T(8,128)(2,1)}, bf16[1280,768]{1,0:T(8,128)(2,1)}, u32[]{:S(2)}, u32[]{:S(2)}) collective-permute-start(bf16[1280,768]{1,0:T(8,128)(2,1)} %get-tuple-element.44), channel_id=1, source_target_pairs={{0,6},{1,7},{2,0},{3,1},{4,2},{5,3},{6,4},{7,5},{8,14},{9,15},{10,... | collective-permute-start | bytes 5898248 | tf_op jit(solution)/shard_map/ppermute | solution.py:328
  156.2 32.3 %copy-start.1 = (bf16[768,768]{1,0:T(8,128)(2,1)}, bf16[768,768]{1,0:T(8,128)(2,1)S(1)}, u32[]{:S(2)}) copy-start(bf16[768,768]{1,0:T(8,128)(2,1)S(1)} %collective-permute-done.14.refs_1_) | copy-start | bytes 3538948
  156.2 43.6 %collective-permute-start.3 = (bf16[1280,768]{1,0:T(8,128)(2,1)}, bf16[1280,768]{1,0:T(8,128)(2,1)}, u32[]{:S(2)}, u32[]{:S(2)}) collective-permute-start(bf16[1280,768]{1,0:T(8,128)(2,1)} %get-tuple-element.45), channel_id=1, source_target_pairs={{0,7},{1,6},{2,1},{3,0},{4,3},{5,2},{6,5},{7,4},{8,15},{9,14},{10,... | collective-permute-start | bytes 5898248 | tf_op jit(solution)/shard_map/ppermute | solution.py:328
  181.0 24.2 %collective-permute-start.4 = (bf16[1280,768]{1,0:T(8,128)(2,1)}, bf16[1280,768]{1,0:T(8,128)(2,1)}, u32[]{:S(2)}, u32[]{:S(2)}) collective-permute-start(bf16[1280,768]{1,0:T(8,128)(2,1)} %get-tuple-element.46), channel_id=1, source_target_pairs={{0,1},{1,0},{2,3},{3,2},{4,5},{5,4},{6,7},{7,6},{8,9},{9,8},{10,11... | collective-permute-start | bytes 5898248 | tf_op jit(solution)/shard_map/ppermute | solution.py:328
  181.0 110.5 %collective-permute-start.5 = (bf16[1280,768]{1,0:T(8,128)(2,1)}, bf16[1280,768]{1,0:T(8,128)(2,1)}, u32[]{:S(2)}, u32[]{:S(2)}) collective-permute-start(bf16[1280,768]{1,0:T(8,128)(2,1)} %get-tuple-element.47), channel_id=1, source_target_pairs={{0,4},{1,5},{2,6},{3,7},{4,0},{5,1},{6,2},{7,3},{8,12},{9,13},{10,... | collective-permute-start | bytes 5898248 | tf_op jit(solution)/shard_map/ppermute | solution.py:328
  184.3 107.2 %collective-permute-start.6 = (bf16[1280,768]{1,0:T(8,128)(2,1)}, bf16[1280,768]{1,0:T(8,128)(2,1)}, u32[]{:S(2)}, u32[]{:S(2)}) collective-permute-start(bf16[1280,768]{1,0:T(8,128)(2,1)} %get-tuple-element.48), channel_id=1, source_target_pairs={{0,5},{1,4},{2,7},{3,6},{4,1},{5,0},{6,3},{7,2},{8,13},{9,12},{10,... | collective-permute-start | bytes 5898248 | tf_op jit(solution)/shard_map/ppermute | solution.py:328
  191.3 200.2 %collective-permute-start.16 = (bf16[768,768]{1,0:T(8,128)(2,1)}, bf16[768,768]{1,0:T(8,128)(2,1)S(1)}, u32[]{:S(2)}, u32[]{:S(2)}) collective-permute-start(bf16[768,768]{1,0:T(8,128)(2,1)} %get-tuple-element.60), channel_id=1, source_target_pairs={{0,6},{1,7},{2,0},{3,1},{4,2},{5,3},{6,4},{7,5},{8,14},{9,15},{10,... | collective-permute-start | bytes 3538952 | tf_op jit(solution)/shard_map/ppermute | solution.py:328
  199.8 191.9 %collective-permute-start.17 = (bf16[768,768]{1,0:T(8,128)(2,1)}, bf16[768,768]{1,0:T(8,128)(2,1)}, u32[]{:S(2)}, u32[]{:S(2)}) collective-permute-start(bf16[768,768]{1,0:T(8,128)(2,1)} %get-tuple-element.61), channel_id=1, source_target_pairs={{0,7},{1,6},{2,1},{3,0},{4,3},{5,2},{6,5},{7,4},{8,15},{9,14},{10,... | collective-permute-start | bytes 3538952 | tf_op jit(solution)/shard_map/ppermute | solution.py:328
  205.2 187.4 %collective-permute-start.18 = (bf16[768,768]{1,0:T(8,128)(2,1)}, bf16[768,768]{1,0:T(8,128)(2,1)}, u32[]{:S(2)}, u32[]{:S(2)}) collective-permute-start(bf16[768,768]{1,0:T(8,128)(2,1)} %get-tuple-element.62), channel_id=1, source_target_pairs={{0,1},{1,0},{2,3},{3,2},{4,5},{5,4},{6,7},{7,6},{8,9},{9,8},{10,11... | collective-permute-start | bytes 3538952 | tf_op jit(solution)/shard_map/ppermute | solution.py:328
  291.5 101.1 %collective-permute-start.19 = (bf16[768,768]{1,0:T(8,128)(2,1)}, bf16[768,768]{1,0:T(8,128)(2,1)}, u32[]{:S(2)}, u32[]{:S(2)}) collective-permute-start(bf16[768,768]{1,0:T(8,128)(2,1)} %get-tuple-element.63), channel_id=1, source_target_pairs={{0,4},{1,5},{2,6},{3,7},{4,0},{5,1},{6,2},{7,3},{8,12},{9,13},{10,... | collective-permute-start | bytes 3538952 | tf_op jit(solution)/shard_map/ppermute | solution.py:328
  291.5 101.1 %collective-permute-start.20 = (bf16[768,768]{1,0:T(8,128)(2,1)}, bf16[768,768]{1,0:T(8,128)(2,1)}, u32[]{:S(2)}, u32[]{:S(2)}) collective-permute-start(bf16[768,768]{1,0:T(8,128)(2,1)} %get-tuple-element.64), channel_id=1, source_target_pairs={{0,5},{1,4},{2,7},{3,6},{4,1},{5,0},{6,3},{7,2},{8,13},{9,12},{10,... | collective-permute-start | bytes 3538952 | tf_op jit(solution)/shard_map/ppermute | solution.py:328
  391.5 1.1 copy-start.3
  391.5 138.8 %collective-permute-start.7 = (bf16[1280,768]{1,0:T(8,128)(2,1)}, bf16[1280,768]{1,0:T(8,128)(2,1)}, u32[]{:S(2)}, u32[]{:S(2)}) collective-permute-start(bf16[1280,768]{1,0:T(8,128)(2,1)} %get-tuple-element.50), channel_id=1, source_target_pairs={{2,0},{3,1},{4,2},{5,3},{6,4},{7,5},{0,6},{1,7},{10,8},{11,9},{12,... | collective-permute-start | bytes 5898248 | tf_op jit(solution)/shard_map/ppermute | solution.py:328
  391.7 138.8 %collective-permute-start.8 = (bf16[1280,768]{1,0:T(8,128)(2,1)}, bf16[1280,768]{1,0:T(8,128)(2,1)}, u32[]{:S(2)}, u32[]{:S(2)}) collective-permute-start(bf16[1280,768]{1,0:T(8,128)(2,1)} %get-tuple-element.51), channel_id=1, source_target_pairs={{3,0},{2,1},{5,2},{4,3},{7,4},{6,5},{1,6},{0,7},{11,8},{10,9},{13,... | collective-permute-start | bytes 5898248 | tf_op jit(solution)/shard_map/ppermute | solution.py:328
  426.9 74.7 %collective-permute-start.21 = (bf16[768,768]{1,0:T(8,128)(2,1)}, bf16[768,768]{1,0:T(8,128)(2,1)S(1)}, u32[]{:S(2)}, u32[]{:S(2)}) collective-permute-start(bf16[768,768]{1,0:T(8,128)(2,1)} %get-tuple-element.66), channel_id=1, source_target_pairs={{2,0},{3,1},{4,2},{5,3},{6,4},{7,5},{0,6},{1,7},{10,8},{11,9},{12,... | collective-permute-start | bytes 3538952 | tf_op jit(solution)/shard_map/ppermute | solution.py:328
  446.4 84.0 %collective-permute-start.22 = (bf16[768,768]{1,0:T(8,128)(2,1)}, bf16[768,768]{1,0:T(8,128)(2,1)}, u32[]{:S(2)}, u32[]{:S(2)}) collective-permute-start(bf16[768,768]{1,0:T(8,128)(2,1)} %get-tuple-element.67), channel_id=1, source_target_pairs={{3,0},{2,1},{5,2},{4,3},{7,4},{6,5},{1,6},{0,7},{11,8},{10,9},{13,... | collective-permute-start | bytes 3538952 | tf_op jit(solution)/shard_map/ppermute | solution.py:328
  446.4 87.3 %collective-permute-start.9 = (bf16[1280,768]{1,0:T(8,128)(2,1)}, bf16[1280,768]{1,0:T(8,128)(2,1)}, u32[]{:S(2)}, u32[]{:S(2)}) collective-permute-start(bf16[1280,768]{1,0:T(8,128)(2,1)} %get-tuple-element.52), channel_id=1, source_target_pairs={{6,0},{7,1},{0,2},{1,3},{2,4},{3,5},{4,6},{5,7},{14,8},{15,9},{8,1... | collective-permute-start | bytes 5898248 | tf_op jit(solution)/shard_map/ppermute | solution.py:328
  501.6 180.5 %copy-start.2 = (bf16[768,768]{1,0:T(8,128)(2,1)}, bf16[768,768]{1,0:T(8,128)(2,1)S(1)}, u32[]{:S(2)}) copy-start(bf16[768,768]{1,0:T(8,128)(2,1)S(1)} %collective-permute-done.21.refs_1_) | copy-start | bytes 3538948
  501.6 49.1 %collective-permute-start.10 = (bf16[1280,768]{1,0:T(8,128)(2,1)}, bf16[1280,768]{1,0:T(8,128)(2,1)}, u32[]{:S(2)}, u32[]{:S(2)}) collective-permute-start(bf16[1280,768]{1,0:T(8,128)(2,1)} %get-tuple-element.53), channel_id=1, source_target_pairs={{7,0},{6,1},{1,2},{0,3},{3,4},{2,5},{5,6},{4,7},{15,8},{14,9},{9,1... | collective-permute-start | bytes 5898248 | tf_op jit(solution)/shard_map/ppermute | solution.py:328
  530.3 109.5 %collective-permute-start.11 = (bf16[1280,768]{1,0:T(8,128)(2,1)}, bf16[1280,768]{1,0:T(8,128)(2,1)}, u32[]{:S(2)}, u32[]{:S(2)}) collective-permute-start(bf16[1280,768]{1,0:T(8,128)(2,1)} %get-tuple-element.54), channel_id=1, source_target_pairs={{1,0},{0,1},{3,2},{2,3},{5,4},{4,5},{7,6},{6,7},{9,8},{8,9},{11,10... | collective-permute-start | bytes 5898248 | tf_op jit(solution)/shard_map/ppermute | solution.py:328
  530.3 109.5 %collective-permute-start.12 = (bf16[1280,768]{1,0:T(8,128)(2,1)}, bf16[1280,768]{1,0:T(8,128)(2,1)}, u32[]{:S(2)}, u32[]{:S(2)}) collective-permute-start(bf16[1280,768]{1,0:T(8,128)(2,1)} %get-tuple-element.55), channel_id=1, source_target_pairs={{4,0},{5,1},{6,2},{7,3},{0,4},{1,5},{2,6},{3,7},{12,8},{13,9},{14,... | collective-permute-start | bytes 5898248 | tf_op jit(solution)/shard_map/ppermute | solution.py:328
  530.5 112.4 %collective-permute-start.13 = (bf16[1280,768]{1,0:T(8,128)(2,1)}, bf16[1280,768]{1,0:T(8,128)(2,1)}, u32[]{:S(2)}, u32[]{:S(2)}) collective-permute-start(bf16[1280,768]{1,0:T(8,128)(2,1)} %get-tuple-element.56), channel_id=1, source_target_pairs={{5,0},{4,1},{7,2},{6,3},{1,4},{0,5},{3,6},{2,7},{13,8},{12,9},{15,... | collective-permute-start | bytes 5898248 | tf_op jit(solution)/shard_map/ppermute | solution.py:328
  533.7 148.3 %collective-permute-start.23 = (bf16[768,768]{1,0:T(8,128)(2,1)}, bf16[768,768]{1,0:T(8,128)(2,1)}, u32[]{:S(2)}, u32[]{:S(2)}) collective-permute-start(bf16[768,768]{1,0:T(8,128)(2,1)} %get-tuple-element.68), channel_id=1, source_target_pairs={{6,0},{7,1},{0,2},{1,3},{2,4},{3,5},{4,6},{5,7},{14,8},{15,9},{8,1... | collective-permute-start | bytes 3538952 | tf_op jit(solution)/shard_map/ppermute | solution.py:328
  550.6 134.8 %collective-permute-start.24 = (bf16[768,768]{1,0:T(8,128)(2,1)}, bf16[768,768]{1,0:T(8,128)(2,1)}, u32[]{:S(2)}, u32[]{:S(2)}) collective-permute-start(bf16[768,768]{1,0:T(8,128)(2,1)} %get-tuple-element.69), channel_id=1, source_target_pairs={{7,0},{6,1},{1,2},{0,3},{3,4},{2,5},{5,6},{4,7},{15,8},{14,9},{9,1... | collective-permute-start | bytes 3538952 | tf_op jit(solution)/shard_map/ppermute | solution.py:328
  639.8 45.7 %collective-permute-start.25 = (bf16[768,768]{1,0:T(8,128)(2,1)}, bf16[768,768]{1,0:T(8,128)(2,1)}, u32[]{:S(2)}, u32[]{:S(2)}) collective-permute-start(bf16[768,768]{1,0:T(8,128)(2,1)} %get-tuple-element.70), channel_id=1, source_target_pairs={{1,0},{0,1},{3,2},{2,3},{5,4},{4,5},{7,6},{6,7},{9,8},{8,9},{11,10... | collective-permute-start | bytes 3538952 | tf_op jit(solution)/shard_map/ppermute | solution.py:328
  639.8 77.4 %collective-permute-start.26 = (bf16[768,768]{1,0:T(8,128)(2,1)}, bf16[768,768]{1,0:T(8,128)(2,1)}, u32[]{:S(2)}, u32[]{:S(2)}) collective-permute-start(bf16[768,768]{1,0:T(8,128)(2,1)} %get-tuple-element.71), channel_id=1, source_target_pairs={{4,0},{5,1},{6,2},{7,3},{0,4},{1,5},{2,6},{3,7},{12,8},{13,9},{14,... | collective-permute-start | bytes 3538952 | tf_op jit(solution)/shard_map/ppermute | solution.py:328
  642.9 97.7 %collective-permute-start.27 = (bf16[768,768]{1,0:T(8,128)(2,1)}, bf16[768,768]{1,0:T(8,128)(2,1)}, u32[]{:S(2)}, u32[]{:S(2)}) collective-permute-start(bf16[768,768]{1,0:T(8,128)(2,1)} %get-tuple-element.72), channel_id=1, source_target_pairs={{5,0},{4,1},{7,2},{6,3},{1,4},{0,5},{3,6},{2,7},{13,8},{12,9},{15,... | collective-permute-start | bytes 3538952 | tf_op jit(solution)/shard_map/ppermute | solution.py:328
